TPU v7x, 256 devices: a whole 4x4x8 slice. The times are simulated.
256 devices in a mesh: row: 32 (over x_hi, z, core), col: 8 (over x_lo, y).
Axes of the slice: x: 4 (x_hi: 2, x_lo: 2; x = x_hi * 2 + x_lo), y: 4, z: 8, core: 2. Of those that a mesh axis runs over, the one named last changes fastest.
Arguments:
- occupied_waves: bfloat16 [1024, 32768], P('row', 'col'), may hold values from -6 to 6
- virtual_waves: bfloat16 [512, 32768], P('row', 'col'), may hold values from -6 to 6
- occupied_decay: float32 [1024], replicated, may hold values from 0.02 to 1
- virtual_decay: float32 [512], replicated, may hold values from 0.02 to 1
Outputs:
- spectrum_real: float32 [1024, 32, 1024], P('row', 'col')
- spectrum_imaginary: float32 [1024, 32, 1024], P('row', 'col')
All inputs are finite; a program needn't handle non-finite values.
Results may differ from a plain program's by a relative error of at most 0.0041.
Values may be sent and summed in bfloat16 or wider, within the bound.
A program may use at most 64 MiB of HBM per device.

v0:
```python
import math

import jax
import jax.numpy as jnp
from jax import lax
from jax.sharding import PartitionSpec as P

NOCC = 1024
NVIR = 512
NA = 32
NB = 32
NC = 32
ROWS_DEV = 32
NGRID = 32768


def sent_to_all(x, axis):
    devices = lax.axis_size(axis)
    return lax.all_to_all(jnp.broadcast_to(x[None], (devices, *x.shape)), axis, 0, 0, tiled=True)


def over_copies(x, axis):
    return sent_to_all(x, axis).astype(jnp.float32).sum(axis=0)


def in_blocks(x, dim, devices):
    shape = x.shape
    parts = x.reshape(*shape[:dim], devices, shape[dim] // devices, *shape[dim + 1 :])
    return jnp.moveaxis(parts, dim, 0)


def laid_out(parts, dim):
    shape = list(parts.shape[1:])
    shape[dim] *= parts.shape[0]
    return jnp.moveaxis(parts, 0, dim).reshape(shape)


def exchange_both(x, axis, axes, splits, concats):
    sizes = [lax.axis_size(a) for a in axes]
    parts = in_blocks(x, splits[0], sizes[0])
    parts = jnp.moveaxis(in_blocks(parts, splits[1] + 1, sizes[1]), 0, 1)
    inside = parts.shape[2:]
    parts = parts.reshape(-1, *inside)
    parts = lax.all_to_all(parts, axis, split_axis=0, concat_axis=0, tiled=True)
    parts = laid_out(parts.reshape(*sizes, *inside), concats[0] + 1)
    return laid_out(parts, concats[1])


def tables(length):
    index = jnp.arange(length, dtype=jnp.int32)
    phase = index[:, None] * index[None, :] % length
    angle = phase.astype(jnp.float32) * (2.0 * math.pi / length)
    return (jnp.cos(angle), jnp.sin(angle))


def apply_table(form, data, table):
    return jnp.einsum(form, data, table, precision=lax.Precision.HIGHEST)


def real_step(data, form, length):
    cosine, sine = tables(length)
    return (apply_table(form, data, cosine), -apply_table(form, data, sine))


def complex_step(real_part, imag_part, form, length):
    cosine, sine = tables(length)
    new_real = apply_table(form, real_part, cosine) + apply_table(form, imag_part, sine)
    new_imag = apply_table(form, imag_part, cosine) - apply_table(form, real_part, sine)
    return (new_real, new_imag)


def scale_rows(waves, decay):
    return (waves * decay[:, None]).astype(jnp.bfloat16)


def place(waves, window, start_col):
    block_cols = waves.shape[1]
    buffer = jnp.zeros((waves.shape[0], window + block_cols), jnp.bfloat16)
    buffer = lax.dynamic_update_slice(buffer, waves, (jnp.int32(0), start_col))
    return buffer[:, :window]


def on_device(occupied_waves, virtual_waves, occupied_decay, virtual_decay):
    block_cols = occupied_waves.shape[1]
    row_count = lax.axis_size("row")
    contract = (((0,), (0,)), ((), ()))
    factor = -1.0 / math.sqrt(NOCC * NVIR)
    window = ROWS_DEV * row_count
    start_col = lax.axis_index("col") * block_cols
    plane_cols = NB * NC
    per_col = block_cols // plane_cols
    spread = row_count // per_col
    sub_rows = ROWS_DEV // spread

    def spread_planes(waves):
        share = waves.shape[0]
        shaped = waves.reshape(share, per_col, 1, plane_cols)
        shaped = jnp.broadcast_to(shaped, (share, per_col, spread, plane_cols))
        return shaped.reshape(share, row_count * plane_cols)

    def pick_rows(waves):
        share = waves.shape[0]
        shaped = place(waves, window, start_col).reshape(share, row_count, spread, sub_rows)
        shaped = jnp.transpose(shaped, (0, 2, 1, 3))[:, None]
        shaped = jnp.broadcast_to(shaped, (share, per_col, spread, row_count, sub_rows))
        return shaped.reshape(share, row_count * row_count * sub_rows)

    plane_occ, plane_vir = (
        lax.all_to_all(
            spread_planes(occupied_waves), "row", split_axis=1, concat_axis=0, tiled=True
        ),
        lax.all_to_all(
            spread_planes(virtual_waves), "row", split_axis=1, concat_axis=0, tiled=True
        ),
    )
    part_occ, part_vir = (
        lax.all_to_all(pick_rows(occupied_waves), "row", split_axis=1, concat_axis=0, tiled=True),
        lax.all_to_all(pick_rows(virtual_waves), "row", split_axis=1, concat_axis=0, tiled=True),
    )
    occ_rows, vir_rows = (
        over_copies(part_occ.astype(jnp.float32).astype(jnp.bfloat16), "col").astype(jnp.float32),
        over_copies(part_vir.astype(jnp.float32).astype(jnp.bfloat16), "col").astype(jnp.float32),
    )
    occ_rows = scale_rows(occ_rows, occupied_decay)
    vir_rows = scale_rows(vir_rows, virtual_decay)
    green_occ = lax.dot_general(plane_occ, occ_rows, contract, preferred_element_type=jnp.float32)
    green_vir = lax.dot_general(plane_vir, vir_rows, contract, preferred_element_type=jnp.float32)
    polar = green_occ * green_vir * factor
    cube = polar.reshape(1, NB, NC, row_count * sub_rows)
    real_part, imag_part = real_step(cube, "abcr,cw->wabr", NC)
    real_part, imag_part = complex_step(real_part, imag_part, "wabr,bv->wavr", NB)
    blocked = (NC, 1, NB, row_count, sub_rows)
    real_part, imag_part = (
        exchange_both(
            real_part.reshape(blocked).astype(jnp.bfloat16),
            ("row", "col"),
            ("row", "col"),
            (3, 0),
            (3, 1),
        ).astype(jnp.float32),
        exchange_both(
            imag_part.reshape(blocked).astype(jnp.bfloat16),
            ("row", "col"),
            ("row", "col"),
            (3, 0),
            (3, 1),
        ).astype(jnp.float32),
    )

    def settle(part):
        kc_share = part.shape[0]
        part = part.reshape(kc_share, part.shape[1], NB, per_col, spread, sub_rows)
        part = jnp.transpose(part, (0, 1, 3, 2, 4, 5))
        return part.reshape(kc_share, NA, NB, ROWS_DEV)

    real_part, imag_part = complex_step(settle(real_part), settle(imag_part), "wavr,au->rwuv", NA)
    normal = 1.0 / math.sqrt(NGRID)
    final_shape = (real_part.shape[0], real_part.shape[1], NA * NB)
    return ((real_part * normal).reshape(final_shape), (imag_part * normal).reshape(final_shape))


def solution(mesh):
    in_specs = (P("row", "col"), P("row", "col"), P(), P())
    out_specs = (P("row", "col", None), P("row", "col", None))
    return jax.shard_map(
        on_device, mesh=mesh, in_specs=in_specs, out_specs=out_specs, check_vma=False
    )
```

profile of v0, /device:TPU:1, one launch (start us, length us, event | category | flops | bytes accessed | tf_op | source)
XLA Modules:
  0.0 266.0 jit_solution(17374565482399408237)
XLA Ops:
  2.6 1.7 copy.78
  4.3 12.6 %all-to-all-start.3 = ((bf16[16,32,128]{2,0,1:T(8,128)(2,1)}), bf16[16,32,128]{2,0,1:T(8,128)(2,1)S(1)}, u32[]{:S(2)}, u32[]{:S(2)}) async-start(bf16[16,32,128]{2,0,1:T(8,128)(2,1)} %copy.78), calls=%async_computation.3 | async-start | bytes 262144 | tf_op jit(solution)/shard_map/all_to_all | solution.py:118
  19.0 8.4 %all-to-all-done.3 = bf16[16,32,128]{2,0,1:T(8,128)(2,1)S(1)} async-done(((bf16[16,32,128]{2,0,1:T(8,128)(2,1)}), bf16[16,32,128]{2,0,1:T(8,128)(2,1)S(1)}, u32[]{:S(2)}, u32[]{:S(2)}) %all-to-all-start.3) | async-done | bytes 131104 | tf_op jit(solution)/shard_map/all_to_all | solution.py:118
  27.4 17.7 %all_to_all.90 = bf16[32,32,128]{2,0,1:T(8,128)(2,1)S(1)} all-to-all(bf16[32,32,128]{2,0,1:T(8,128)(2,1)S(1)} %copy.74), channel_id=1, replica_groups=mesh['row'=32,'col'=8] {'row'}, dimensions={1} | all-to-all | bytes 524288 | tf_op jit(solution)/shard_map/all_to_all | solution.py:117
  45.2 16.9 %all_to_all.91 = bf16[8,512,128]{2,1,0:T(8,128)(2,1)S(1)} all-to-all(bf16[8,512,128]{2,1,0:T(8,128)(2,1)S(1)} %broadcast_in_dim.65), channel_id=1, replica_groups=mesh['row'=32,'col'=8] {'col'}, dimensions={0} | all-to-all | bytes 2097152 | tf_op jit(solution)/shard_map/all_to_all | solution.py:19
  63.8 4.2 %all-to-all-start.1 = ((bf16[8,1024,128]{2,1,0:T(8,128)(2,1)}), bf16[8,1024,128]{2,1,0:T(8,128)(2,1)S(1)}, u32[]{:S(2)}, u32[]{:S(2)}) async-start(bf16[8,1024,128]{2,1,0:T(8,128)(2,1)} %broadcast_in_dim.27), calls=%async_computation.1 | async-start | bytes 4194304 | tf_op jit(solution)/shard_map/all_to_all | solution.py:19
  68.6 25.2 %all-to-all-done.1 = bf16[8,1024,128]{2,1,0:T(8,128)(2,1)S(1)} async-done(((bf16[8,1024,128]{2,1,0:T(8,128)(2,1)}), bf16[8,1024,128]{2,1,0:T(8,128)(2,1)S(1)}, u32[]{:S(2)}, u32[]{:S(2)}) %all-to-all-start.1) | async-done | bytes 2097184 | tf_op jit(solution)/shard_map/all_to_all | solution.py:19
  93.8 2.5 broadcast_in_dim.29
  96.4 6.1 %all-to-all-start.2 = ((bf16[32,32,1024]{2,0,1:T(8,128)(2,1)}), bf16[32,32,1024]{2,0,1:T(8,128)(2,1)}, u32[]{:S(2)}, u32[]{:S(2)}) async-start(bf16[32,32,1024]{2,0,1:T(8,128)(2,1)} %bitcast.125), calls=%async_computation.2 | async-start | bytes 4194304 | tf_op jit(solution)/shard_map/all_to_all | solution.py:109
  102.5 50.8 %all-to-all-done.2 = bf16[32,32,1024]{2,0,1:T(8,128)(2,1)} async-done(((bf16[32,32,1024]{2,0,1:T(8,128)(2,1)}), bf16[32,32,1024]{2,0,1:T(8,128)(2,1)}, u32[]{:S(2)}, u32[]{:S(2)}) %all-to-all-start.2) | async-done | bytes 2097184 | tf_op jit(solution)/shard_map/all_to_all | solution.py:109
  154.4 5.7 %all-to-all-start.5 = ((bf16[16,32,1024]{2,0,1:T(8,128)(2,1)}), bf16[16,32,1024]{2,0,1:T(8,128)(2,1)}, u32[]{:S(2)}, u32[]{:S(2)}) async-start(bf16[16,32,1024]{2,0,1:T(8,128)(2,1)} %bitcast.136), calls=%async_computation.5 | async-start | bytes 2097152 | tf_op jit(solution)/shard_map/all_to_all | solution.py:112
  160.8 2.3 fusion.12
  163.2 24.4 %all-to-all-done.5 = bf16[16,32,1024]{2,0,1:T(8,128)(2,1)} async-done(((bf16[16,32,1024]{2,0,1:T(8,128)(2,1)}), bf16[16,32,1024]{2,0,1:T(8,128)(2,1)}, u32[]{:S(2)}, u32[]{:S(2)}) %all-to-all-start.5) | async-done | bytes 1048608 | tf_op jit(solution)/shard_map/all_to_all | solution.py:112
  195.9 8.5 %all-to-all-start.7 = ((bf16[256,2,256]{2,1,0:T(2,128)(2,1)}), bf16[256,2,256]{2,1,0:T(2,128)(2,1)S(1)}, u32[]{:S(2)}, u32[]{:S(2)}) async-start(bf16[256,2,256]{2,1,0:T(2,128)(2,1)} %reshape.155), calls=%async_computation.7 | async-start | bytes 524288 | tf_op jit(solution)/shard_map/all_to_all | solution.py:44
  209.5 10.1 %all-to-all-done.7 = bf16[256,2,256]{2,1,0:T(2,128)(2,1)S(1)} async-done(((bf16[256,2,256]{2,1,0:T(2,128)(2,1)}), bf16[256,2,256]{2,1,0:T(2,128)(2,1)S(1)}, u32[]{:S(2)}, u32[]{:S(2)}) %all-to-all-start.7) | async-done | bytes 262176 | tf_op jit(solution)/shard_map/all_to_all | solution.py:44
  219.6 5.7 %all-to-all-start.6 = ((bf16[256,2,256]{2,1,0:T(2,128)(2,1)}), bf16[256,2,256]{2,1,0:T(2,128)(2,1)S(1)}, u32[]{:S(2)}, u32[]{:S(2)}) async-start(bf16[256,2,256]{2,1,0:T(2,128)(2,1)} %reshape.153), calls=%async_computation.6 | async-start | bytes 524288 | tf_op jit(solution)/shard_map/all_to_all | solution.py:44
  228.6 12.0 %all-to-all-done.6 = bf16[256,2,256]{2,1,0:T(2,128)(2,1)S(1)} async-done(((bf16[256,2,256]{2,1,0:T(2,128)(2,1)}), bf16[256,2,256]{2,1,0:T(2,128)(2,1)S(1)}, u32[]{:S(2)}, u32[]{:S(2)}) %all-to-all-start.6) | async-done | bytes 262176 | tf_op jit(solution)/shard_map/all_to_all | solution.py:44
  245.0 2.4 fusion.20
  247.3 2.4 multiply_bitcast_fusion.1
  249.8 4.1 %copy.105 = f32[32,4,32,32]{3,2,1,0:T(8,128)} copy(f32[32,4,32,32]{0,2,3,1:T(8,128)} %multiply_bitcast_fusion.1) | data formatting | bytes 1048576
  253.8 3.1 %reshape.151 = f32[32,4,1024]{2,1,0:T(4,128)} reshape(f32[32,4,32,32]{3,2,1,0:T(8,128)} %copy.105) | data formatting | bytes 1048576
  257.0 4.0 %multiply_bitcast_fusion = f32[32,4,32,32]{0,2,3,1:T(8,128)} fusion(f32[32,4,32,32]{3,0,2,1:T(8,128)} %fusion.20, bf16[4,32,32,32]{3,1,2,0:T(8,128)(2,1)S(1)} %copy.88), kind=kOutput, calls=%fused_computation.1 | convolution fusion | flops 50608128 | bytes 1310720 | tf_op jit(solution)/shard_map/wavr,au->rwuv/dot_general | solution.py:57
  261.0 3.2 %copy.106 = f32[32,4,32,32]{3,2,1,0:T(8,128)S(1)} copy(f32[32,4,32,32]{0,2,3,1:T(8,128)} %multiply_bitcast_fusion) | data formatting | bytes 1048576
  264.2 1.7 reshape.152
  (53 shorter events, 29.2 us)
Async XLA Ops:
  2.4 14.5 %copy-start = (bf16[32,4096]{1,0:T(8,128)(2,1)S(1)}, bf16[32,4096]{1,0:T(8,128)(2,1)}, u32[]{:S(2)}) copy-start(bf16[32,4096]{1,0:T(8,128)(2,1)} %param.4) | copy-start | bytes 786436
  4.3 23.1 %all-to-all-start.3 = ((bf16[16,32,128]{2,0,1:T(8,128)(2,1)}), bf16[16,32,128]{2,0,1:T(8,128)(2,1)S(1)}, u32[]{:S(2)}, u32[]{:S(2)}) async-start(bf16[16,32,128]{2,0,1:T(8,128)(2,1)} %copy.78), calls=%async_computation.3 | async-start | bytes 262144 | tf_op jit(solution)/shard_map/all_to_all | solution.py:118
  63.8 30.1 %all-to-all-start.1 = ((bf16[8,1024,128]{2,1,0:T(8,128)(2,1)}), bf16[8,1024,128]{2,1,0:T(8,128)(2,1)S(1)}, u32[]{:S(2)}, u32[]{:S(2)}) async-start(bf16[8,1024,128]{2,1,0:T(8,128)(2,1)} %broadcast_in_dim.27), calls=%async_computation.1 | async-start | bytes 4194304 | tf_op jit(solution)/shard_map/all_to_all | solution.py:19
  96.4 6.1 %copy-start.1 = (bf16[16,4096]{1,0:T(8,128)(2,1)S(1)}, bf16[16,4096]{1,0:T(8,128)(2,1)}, u32[]{:S(2)}) copy-start(bf16[16,4096]{1,0:T(8,128)(2,1)} %param.5) | copy-start | bytes 393220
  96.4 57.0 %all-to-all-start.2 = ((bf16[32,32,1024]{2,0,1:T(8,128)(2,1)}), bf16[32,32,1024]{2,0,1:T(8,128)(2,1)}, u32[]{:S(2)}, u32[]{:S(2)}) async-start(bf16[32,32,1024]{2,0,1:T(8,128)(2,1)} %bitcast.125), calls=%async_computation.2 | async-start | bytes 4194304 | tf_op jit(solution)/shard_map/all_to_all | solution.py:109
  154.4 33.1 %all-to-all-start.5 = ((bf16[16,32,1024]{2,0,1:T(8,128)(2,1)}), bf16[16,32,1024]{2,0,1:T(8,128)(2,1)}, u32[]{:S(2)}, u32[]{:S(2)}) async-start(bf16[16,32,1024]{2,0,1:T(8,128)(2,1)} %bitcast.136), calls=%async_computation.5 | async-start | bytes 2097152 | tf_op jit(solution)/shard_map/all_to_all | solution.py:112
  160.1 0.7 copy-start.2
  160.6 27.0 %copy-start.3 = (f32[512]{0:T(512)S(1)}, f32[512]{0:T(512)}, u32[]{:S(2)}) copy-start(f32[512]{0:T(512)} %param.7) | copy-start | bytes 6148
  195.9 23.7 %all-to-all-start.7 = ((bf16[256,2,256]{2,1,0:T(2,128)(2,1)}), bf16[256,2,256]{2,1,0:T(2,128)(2,1)S(1)}, u32[]{:S(2)}, u32[]{:S(2)}) async-start(bf16[256,2,256]{2,1,0:T(2,128)(2,1)} %reshape.155), calls=%async_computation.7 | async-start | bytes 524288 | tf_op jit(solution)/shard_map/all_to_all | solution.py:44
  219.6 21.0 %all-to-all-start.6 = ((bf16[256,2,256]{2,1,0:T(2,128)(2,1)}), bf16[256,2,256]{2,1,0:T(2,128)(2,1)S(1)}, u32[]{:S(2)}, u32[]{:S(2)}) async-start(bf16[256,2,256]{2,1,0:T(2,128)(2,1)} %reshape.153), calls=%async_computation.6 | async-start | bytes 524288 | tf_op jit(solution)/shard_map/all_to_all | solution.py:44
where the time goes:
time: 267 us; the launch traced here: 266 us
  waiting for transfers between devices  131 us (49%)
  starting transfers between devices  42.8 us (16%)
  local copies, waits for them, and re-layouts  37.5 us (14%)
  blocking collectives  34.6 us (13%)
  matrix products  18.8 us (7%)
    all_to_all x1, waiting for transfers between devices, on_device(): lax.all_to_all(spread_planes(occupied_waves), 'row', split_axis=1, concat...  50.8 us
    all_to_all x1, waiting for transfers between devices, sent_to_all(): lax.all_to_all(jnp.broadcast_to(x[None], (devices, *x.shape)), axis, 0, 0...  25.2 us
    all_to_all x1, waiting for transfers between devices, on_device(): lax.all_to_all(spread_planes(virtual_waves), 'row', split_axis=1, concat_...  24.4 us
    all_to_all x2, waiting for transfers between devices, exchange_both(): parts = lax.all_to_all(parts, axis, split_axis=0, concat_axis=0, tiled=True)  22 us
    unnamed x18, local copies, waits for them, and re-layouts  18 us
    all_to_all x1, blocking collectives, on_device(): lax.all_to_all(pick_rows(occupied_waves), 'row', split_axis=1, concat_axi...  17.7 us
    all_to_all x1, blocking collectives, sent_to_all(): lax.all_to_all(jnp.broadcast_to(x[None], (devices, *x.shape)), axis, 0, 0...  16.9 us
    dot_general x10, matrix products, apply_table(): return jnp.einsum(form, data, table, precision=lax.Precision.HIGHEST)  14.8 us
  transfers between devices with their start and end apart: 6, of which 6 were waited for; matrix products, arithmetic and copies ran while one was open for 5% of the time, Pallas kernels for 0%

commit v1 on v0

v1 whole, which is shorter than its diff:
```python
import functools
import math

import jax
import jax.numpy as jnp
import numpy as np
from jax import lax
from jax.experimental import pallas as pl
from jax.experimental.pallas import tpu as pltpu
from jax.sharding import PartitionSpec as P

MESH = pl.DeviceIdType.MESH
F32 = jnp.float32
BF16 = jnp.bfloat16
SCALE = -(2.0**-17)
DIST = (1, 7, 2, 6, 3, 5, 4)


def angle_table(length):
    k = np.arange(length)
    phase = np.outer(k, k) % length
    angle = 2.0 * np.pi * phase / length
    return np.cos(angle), np.sin(angle)


def c_table():
    cos, sin = angle_table(32)
    cos, sin = cos.reshape(32, 8, 1, 4), -sin.reshape(32, 8, 1, 4)
    both = np.stack([cos, sin], axis=2)
    return np.broadcast_to(both, (32, 8, 2, 16, 4)).reshape(32, 1024).astype(np.float32)


def b_table():
    cos, sin = angle_table(32)
    table = np.zeros((2, 2, 16, 4, 2, 4, 32), np.float32)
    for kc in range(4):
        c = cos.reshape(2, 16, 32)
        s = sin.reshape(2, 16, 32)
        table[:, 0, :, kc, 0, kc, :] = c
        table[:, 0, :, kc, 1, kc, :] = -s
        table[:, 1, :, kc, 0, kc, :] = s
        table[:, 1, :, kc, 1, kc, :] = c
    return table.reshape(256, 256)


def fft(parts):
    n = len(parts)
    if n == 1:
        return parts
    half = n // 2
    even, odd = fft(parts[0::2]), fft(parts[1::2])
    low, high = [], []
    for k in range(half):
        (ar, ai), (br, bi) = even[k], odd[k]
        if k == 0:
            tr, ti = br, bi
        elif 4 * k == n:
            tr, ti = bi, -br
        else:
            c, s = math.cos(2 * math.pi * k / n), math.sin(2 * math.pi * k / n)
            tr, ti = c * br + s * bi, c * bi - s * br
        low.append((ar + tr, ai + ti))
        high.append((ar - tr, ai - ti))
    return low + high


def swap_groups(v, lane):
    v = list(v)
    for shift, pairs in ((64, ((0, 2), (1, 3))), (32, ((0, 1), (2, 3)))):
        low = lax.rem(lane, 2 * shift) < shift
        for i, j in pairs:
            a, b = v[i], v[j]
            v[i] = jnp.where(low, a, pltpu.roll(b, shift, 1))
            v[j] = jnp.where(low, pltpu.roll(a, 128 - shift, 1), b)
    return v


def tdot(a, b):
    return lax.dot_general(a, b, (((0,), (0,)), ((), ())), preferred_element_type=F32)


def mdot(a, b):
    return jnp.dot(a, b, preferred_element_type=F32)


def kernel(
    occ, vir, docc, dvir, ctab, btab, out_re, out_im,
    inb, dov, dvv, ctv, btv, mhi, mlo, nhi, nlo,
    pz, pb, rs, ra, rb, rc, yb, xr, zb,
    in_sem, p1s, p1r, p2s, p2r, p3s, p3r, ras, rar, rbs, rbr, rcs, rcr, ys, yr,
):
    row, col = lax.axis_index("row"), lax.axis_index("col")
    core = lax.rem(row, 2)
    z = lax.rem(lax.div(row, 2), 8)
    xh = lax.div(row, 16)
    y, xl = lax.rem(col, 4), lax.div(col, 4)
    x = 2 * xh + xl

    def row_of(xh_, z_, k_):
        return (xh_ * 8 + z_) * 2 + k_

    loads = [
        pltpu.make_async_copy(occ, inb.at[pl.ds(0, 32)], in_sem.at[0]),
        pltpu.make_async_copy(vir, inb.at[pl.ds(32, 16)], in_sem.at[1]),
        pltpu.make_async_copy(docc, dov, in_sem.at[2]),
        pltpu.make_async_copy(dvir, dvv, in_sem.at[3]),
        pltpu.make_async_copy(ctab, ctv, in_sem.at[4]),
        pltpu.make_async_copy(btab, btv, in_sem.at[5]),
    ]
    for load in loads:
        load.start()

    barrier = pltpu.get_barrier_semaphore()

    def greet(i, c):
        pl.semaphore_signal(
            barrier, inc=1, device_id=(xh * 16 + lax.div(i, 8), lax.rem(i, 8)), device_id_type=MESH
        )
        return c

    lax.fori_loop(0, 128, greet, 0)

    def greet_other(i, c):
        pl.semaphore_signal(
            barrier, inc=1, device_id=(row_of(1 - xh, z, core), i), device_id_type=MESH
        )
        return c

    lax.fori_loop(0, 8, greet_other, 0)

    for load in loads:
        load.wait()

    @pl.when(col == 0)
    def _():
        lane = lax.broadcasted_iota(jnp.int32, (32, 1024), 1)
        band = lax.broadcasted_iota(jnp.int32, (32, 1024), 0)
        dec = jnp.sum(jnp.where(lane == band + 32 * row, dov[...], 0.0), axis=1, keepdims=True)
        rs[0:32, :] = (inb[0:32, 0:1024].astype(F32) * dec).astype(BF16)
        lane = lax.broadcasted_iota(jnp.int32, (16, 512), 1)
        band = lax.broadcasted_iota(jnp.int32, (16, 512), 0)
        dec = jnp.sum(jnp.where(lane == band + 16 * row, dvv[...], 0.0), axis=1, keepdims=True)
        rs[32:48, :] = (inb[32:48, 0:1024].astype(F32) * dec).astype(BF16)

    pl.semaphore_wait(barrier, 136)

    def a_copy(s, c):
        lanes = pl.ds(pl.multiple_of(512 * s + 128 * lax.rem(c, 4), 128), 128)
        return pltpu.make_async_remote_copy(
            src_ref=rs.at[:, lanes], dst_ref=ra.at[xh], send_sem=ras.at[s, c], recv_sem=rar.at[xh],
            device_id=(row_of(s, z, core), c), device_id_type=MESH,
        )

    def a_wait(xs):
        pltpu.make_async_copy(ra.at[xs], ra.at[xs], rar.at[xs]).wait()

    def p1_copy(dz):
        zt = lax.rem(z + dz, 8)
        lanes = pl.ds(pl.multiple_of(zt * 512, 512), 512)
        return pltpu.make_async_remote_copy(
            src_ref=inb.at[:, lanes], dst_ref=pz.at[z], send_sem=p1s.at[dz], recv_sem=p1r.at[z],
            device_id=(row_of(xh, zt, core), col), device_id_type=MESH,
        )

    def p1_wait(zs):
        pltpu.make_async_copy(pz.at[zs], pz.at[zs], p1r.at[zs]).wait()

    def b_copy(dz):
        zt = lax.rem(z + dz, 8)
        return pltpu.make_async_remote_copy(
            src_ref=ra, dst_ref=rb.at[z], send_sem=rbs.at[dz], recv_sem=rbr.at[z],
            device_id=(row_of(xh, zt, core), col), device_id_type=MESH,
        )

    def b_wait(zs):
        pltpu.make_async_copy(rb.at[zs], rb.at[zs], rbr.at[zs]).wait()

    def p2_copy(src, zs, side):
        xt = lax.rem(x + 1 + 2 * side, 4)
        return pltpu.make_async_remote_copy(
            src_ref=src, dst_ref=pb.at[xh, core, zs], send_sem=p2s.at[side, zs], recv_sem=p2r.at[xh, zs],
            device_id=(row_of(lax.div(xt, 2), z, core), lax.rem(xt, 2) * 4 + y), device_id_type=MESH,
        )

    def p2_wait(xs, zs):
        pltpu.make_async_copy(pb.at[xs, core, zs], pb.at[xs, core, zs], p2r.at[xs, zs]).wait()

    def p3_copy(xs, zs):
        return pltpu.make_async_remote_copy(
            src_ref=pb.at[xs, core, zs], dst_ref=pb.at[xs, core, zs], send_sem=p3s.at[xs, zs],
            recv_sem=p3r.at[xs, zs], device_id=(row + 1 - 2 * core, col), device_id_type=MESH,
        )

    def p3_wait(xs, zs):
        other = 1 - core
        pltpu.make_async_copy(pb.at[xs, other, zs], pb.at[xs, other, zs], p3r.at[xs, zs]).wait()

    def c_copy(zs, yt):
        return pltpu.make_async_remote_copy(
            src_ref=rb.at[zs], dst_ref=rc.at[lax.rem(y, 2), core, zs], send_sem=rcs.at[yt, zs],
            recv_sem=rcr.at[lax.rem(y, 2), core, zs],
            device_id=(row_of(xh, z, lax.div(y, 2)), xl * 4 + yt), device_id_type=MESH,
        )

    def c_wait(yp, ks, zs):
        pltpu.make_async_copy(rc.at[yp, ks, zs], rc.at[yp, ks, zs], rcr.at[yp, ks, zs]).wait()

    own_half = core == lax.div(y, 2)

    @pl.when(col == 0)
    def _():
        def send(i, carry):
            s, c = lax.div(i, 8), lax.rem(i, 8)

            @pl.when(jnp.logical_or(s != xh, c != 0))
            def _():
                a_copy(s, c).start()

            return carry

        lax.fori_loop(0, 16, send, 0)
        ra[xh] = rs[:, pl.ds(pl.multiple_of(512 * xh, 512), 128)]

    for dz in DIST[:2]:
        p1_copy(dz).start()

    mine = pl.ds(pl.multiple_of(z * 512, 512), 512)
    for side in range(2):
        p2_copy(inb.at[:, mine], z, side).start()

    for xs in range(2):
        @pl.when(jnp.logical_or(col != 0, xh != xs))
        def _():
            a_wait(xs)

    for dz in DIST:
        b_copy(dz).start()
    for dz in DIST[2:]:
        p1_copy(dz).start()

    blane = lax.rem(lax.div(lax.broadcasted_iota(jnp.int32, (32, 1024), 1), 4), 16)
    ct = ctv[...]
    ct_hi = ct.astype(BF16).astype(F32)
    ct_lo = ct - ct_hi

    def table(b, c):
        rows = pl.ds(pl.multiple_of(b * 32, 32), 32)
        mhi[rows, :] = jnp.where(blane == b, ct_hi, 0.0).astype(BF16)
        mlo[rows, :] = jnp.where(blane == b, ct_lo, 0.0).astype(BF16)
        return c

    lax.fori_loop(0, 16, table, 0)
    bt = btv[...]
    bt_hi = bt.astype(BF16)
    nhi[...] = bt_hi
    nlo[...] = (bt - bt_hi.astype(F32)).astype(BF16)

    rb[z] = ra[...]

    def c_sends(zs):
        def one(yt, carry):
            @pl.when(jnp.logical_or(yt != y, jnp.logical_not(own_half)))
            def _():
                c_copy(zs, yt).start()

            return carry

        lax.fori_loop(0, 4, one, 0)

        @pl.when(own_half)
        def _():
            rc[lax.rem(y, 2), core, zs] = rb[zs]

    c_sends(z)

    def step(i, carry):
        dz = lax.rem(i, 2) * lax.div(i + 1, 2) + (1 - lax.rem(i, 2)) * (8 - lax.div(i, 2))
        zs = lax.rem(z + 8 - dz, 8)
        p1_wait(zs)
        p2_copy(pz.at[zs], zs, 0).start()
        p2_copy(pz.at[zs], zs, 1).start()
        b_wait(zs)
        c_sends(zs)
        return carry

    lax.fori_loop(1, 8, step, 0)

    def forward(i, carry):
        dz = lax.rem(i, 2) * lax.div(i + 1, 2) + (1 - lax.rem(i, 2)) * lax.rem(8 - lax.div(i, 2), 8)
        zs = lax.rem(z + 8 - dz, 8)
        for xs in range(2):
            p2_wait(xs, zs)
            p3_copy(xs, zs).start()
        return carry

    lax.fori_loop(0, 8, forward, 0)

    def arrive(zs, carry):
        for xs in range(2):
            p3_wait(xs, zs)
        for yp in range(2):
            for ks in range(2):
                @pl.when(jnp.logical_or(y != 2 * core + yp, ks != core))
                def _():
                    c_wait(yp, ks, zs)
        return carry

    lax.fori_loop(0, 8, arrive, 0)

    for yp in range(2):
        acc_o = jnp.zeros((128, 512), F32)
        acc_v = jnp.zeros((128, 512), F32)
        for xs in range(2):
            for ks in range(2):
                acc_o += tdot(
                    rc[yp, ks, :, xs, 0:32, :].reshape(256, 128), pb[xs, ks, :, 0:32, :].reshape(256, 512)
                )
                acc_v += tdot(
                    rc[yp, ks, :, xs, 32:48, :].reshape(128, 128), pb[xs, ks, :, 32:48, :].reshape(128, 512)
                )
        polar = acc_o * acc_v * SCALE
        hi = polar.astype(BF16)
        lo = (polar - hi.astype(F32)).astype(BF16)
        yb[128 * yp : 128 * yp + 128, :] = (mdot(hi, mhi[...]) + mdot(hi, mlo[...]) + mdot(lo, mhi[...])).astype(BF16)

    slot = ((1 - xl) * 4 + y) * 8 + z
    has_self = lax.div(z, 4) == core

    def y_copy(m, c):
        rows = pl.ds(pl.multiple_of(m * 32, 32), 32)
        lanes = pl.ds(pl.multiple_of(c * 128, 128), 128)
        return pltpu.make_async_remote_copy(
            src_ref=yb.at[rows, lanes], dst_ref=xr.at[slot], send_sem=ys, recv_sem=yr,
            device_id=(16 * xh + 8 * core + m, c), device_id_type=MESH,
        )

    def y_send(i, carry):
        m = lax.rem(lax.div(i, 8) + 2 * z, 8)
        c = lax.rem(lax.rem(i, 8) + col, 8)

        @pl.when(jnp.logical_or(16 * xh + 8 * core + m != row, c != col))
        def _():
            y_copy(m, c).start()

        return carry

    lax.fori_loop(0, 64, y_send, 0)

    @pl.when(has_self)
    def _():
        m = row - 16 * xh - 8 * core
        xr[slot] = yb[pl.ds(pl.multiple_of(m * 32, 32), 32), pl.ds(pl.multiple_of(col * 128, 128), 128)]
        pltpu.make_async_copy(xr.at[pl.ds(0, 63)], xr.at[pl.ds(0, 63)], yr).wait()

    @pl.when(jnp.logical_not(has_self))
    def _():
        pltpu.make_async_copy(xr, xr, yr).wait()

    def b_step(i, carry):
        part = xr[pl.ds(pl.multiple_of(8 * i, 8), 8)].reshape(4, 2, 32, 128)
        both = jnp.concatenate([part[:, 0].reshape(128, 128), part[:, 1].reshape(128, 128)], axis=1)
        res = mdot(both, nhi[...]) + mdot(both, nlo[...])
        zb[pl.ds(4 * i, 4)] = res.reshape(4, 32, 256)
        return carry

    lax.fori_loop(0, 8, b_step, 0)

    lane = lax.broadcasted_iota(jnp.int32, (8, 128), 1)

    def a_step(i, carry):
        rows = pl.ds(pl.multiple_of(8 * i, 8), 8)
        res = fft([(zb[a, rows, 0:128], zb[a, rows, 128:256]) for a in range(32)])
        for j in range(8):
            for part, out in ((0, out_re), (1, out_im)):
                moved = swap_groups([res[4 * j + t][part] for t in range(4)], lane)
                for kc in range(4):
                    out[pl.ds(i * 256 + j * 4 + kc, 8, stride=32), :] = moved[kc]
        return carry

    lax.fori_loop(0, 4, a_step, 0)

    @pl.when(col == 0)
    def _():
        def sent(i, carry):
            s, c = lax.div(i, 8), lax.rem(i, 8)

            @pl.when(jnp.logical_or(s != xh, c != 0))
            def _():
                a_copy(s, c).wait_send()

            return carry

        lax.fori_loop(0, 16, sent, 0)

    def sent_z(dz, carry):
        p1_copy(dz).wait_send()
        b_copy(dz).wait_send()
        return carry

    lax.fori_loop(1, 8, sent_z, 0)

    def sent_zs(zs, carry):
        for side in range(2):
            p2_copy(pz.at[zs], zs, side).wait_send()
            p3_copy(side, zs).wait_send()

        def one(yt, c):
            @pl.when(jnp.logical_or(yt != y, jnp.logical_not(own_half)))
            def _():
                c_copy(zs, yt).wait_send()

            return c

        return lax.fori_loop(0, 4, one, carry)

    lax.fori_loop(0, 8, sent_zs, 0)

    @pl.when(has_self)
    def _():
        pltpu.make_async_copy(xr.at[pl.ds(0, 63)], xr.at[pl.ds(0, 63)], ys).wait()

    @pl.when(jnp.logical_not(has_self))
    def _():
        pltpu.make_async_copy(xr, xr, ys).wait()


def on_device(occ, vir, docc, dvir):
    anyspace = pl.BlockSpec(memory_space=pl.ANY)
    vmem = pl.BlockSpec(memory_space=pltpu.VMEM)
    dma = pltpu.SemaphoreType.DMA
    out = jax.ShapeDtypeStruct((1024, 128), F32)
    res = pl.pallas_call(
        kernel,
        out_shape=(out, out),
        in_specs=[anyspace] * 6,
        out_specs=(vmem, vmem),
        scratch_shapes=[
            pltpu.VMEM((48, 4096), BF16),
            pltpu.VMEM((1, 1024), F32),
            pltpu.VMEM((1, 512), F32),
            pltpu.VMEM((32, 1024), F32),
            pltpu.VMEM((256, 256), F32),
            pltpu.VMEM((512, 1024), BF16),
            pltpu.VMEM((512, 1024), BF16),
            pltpu.VMEM((256, 256), BF16),
            pltpu.VMEM((256, 256), BF16),
            pltpu.VMEM((8, 48, 512), BF16),
            pltpu.VMEM((2, 2, 8, 48, 512), BF16),
            pltpu.VMEM((48, 1024), BF16),
            pltpu.VMEM((2, 48, 128), BF16),
            pltpu.VMEM((8, 2, 48, 128), BF16),
            pltpu.VMEM((2, 2, 8, 2, 48, 128), BF16),
            pltpu.VMEM((256, 1024), BF16),
            pltpu.VMEM((64, 32, 128), BF16),
            pltpu.VMEM((32, 32, 256), F32),
            dma((6,)),
            dma((8,)), dma((8,)),
            dma((2, 8)), dma((2, 8)),
            dma((2, 8)), dma((2, 8)),
            dma((2, 8)), dma((2,)),
            dma((8,)), dma((8,)),
            dma((4, 8)), dma((2, 2, 8)),
            dma, dma,
        ],
        compiler_params=pltpu.CompilerParams(collective_id=0, has_side_effects=True),
    )(
        occ, vir, docc.reshape(1, 1024), dvir.reshape(1, 512),
        jnp.asarray(c_table()), jnp.asarray(b_table()),
    )

    def placed(part):
        return jnp.transpose(part.reshape(32, 8, 4, 128), (0, 2, 1, 3)).reshape(32, 4, 1024)

    return placed(res[0]), placed(res[1])


def solution(mesh):
    in_specs = (P("row", "col"), P("row", "col"), P(), P())
    out_specs = (P("row", "col", None), P("row", "col", None))
    return jax.shard_map(
        on_device, mesh=mesh, in_specs=in_specs, out_specs=out_specs, check_vma=False
    )
```

time: 267 us -> 62.9 us (0.24)
  waiting for transfers between devices: 131 us -> 0 us
  Pallas kernels: 0 us -> 59.4 us
  starting transfers between devices: 42.8 us -> 0 us
  local copies, waits for them, and re-layouts: 37.5 us -> 2.72 us
  blocking collectives: 34.6 us -> 0 us
  matrix products: 18.8 us -> 0 us
    all_to_all x6 -> x0, waiting for transfers between devices: 131 us -> none  [the longest x1 50.8 us: on_device(): lax.all_to_all(spread_planes(occupied_waves), 'row', split_axis=1, concat...]
    pallas_call x0 -> x1, Pallas kernels: none -> 59.4 us  [on_device(): pl.pallas_call(kernel, out_shape=(out, out), in_specs=[anyspace] * 6, out...]
    all_to_all x6 -> x0, starting transfers between devices: 42.8 us -> none  [the longest x2 14.2 us: exchange_both(): parts = lax.all_to_all(parts, axis, split_axis=0, concat_axis=0, tiled=True)]
    all_to_all x2 -> x0, blocking collectives: 34.6 us -> none  [the longest x1 17.7 us: on_device(): lax.all_to_all(pick_rows(occupied_waves), 'row', split_axis=1, concat_axi...]
    dot_general x12 -> x0, matrix products: 18.8 us -> none  [the longest x10 14.8 us: apply_table(): return jnp.einsum(form, data, table, precision=lax.Precision.HIGHEST)]
    unnamed x18 -> x4, local copies, waits for them, and re-layouts: 18 us -> 2.72 us
    broadcast_in_dim x10 -> x0, local copies, waits for them, and re-layouts: 6.74 us -> none  [the longest x4 4.38 us: spread_planes(): shaped = jnp.broadcast_to(shaped, (share, per_col, spread, plane_cols))]
    reshape x4 -> x0, local copies, waits for them, and re-layouts: 5.03 us -> none  [the longest x2 3.4 us: settle(): return part.reshape(kc_share, NA, NB, ROWS_DEV)]
  transfers between devices with their start and end apart: 6 -> 0, of which waited for: 6 -> 0; matrix products, arithmetic and copies ran while one was open for 5% -> 0% of each run, Pallas kernels for 0% -> 0%
where the time goes in v1:
time: 62.9 us; the launch traced here: 62.8 us
  Pallas kernels  59.4 us (94%)
  local copies, waits for them, and re-layouts  2.72 us (4%)
  between operations  0.65 us (1%)
    pallas_call x1, Pallas kernels, on_device(): pl.pallas_call(kernel, out_shape=(out, out), in_specs=[anyspace] * 6, out...  59.4 us
    unnamed x4, local copies, waits for them, and re-layouts  2.72 us

profile of v1, /device:TPU:1, one launch (start us, length us, event | category | flops | bytes accessed | tf_op | source)
XLA Modules:
  0.0 62.8 jit_solution(5678187135627482412)
XLA Ops:
  0.6 59.4 %shard_map.77 = (f32[1024,128]{1,0:T(8,128)}, f32[1024,128]{1,0:T(8,128)}) custom-call(bf16[32,4096]{1,0:T(8,128)(2,1)} %occ.1, bf16[16,4096]{1,0:T(8,128)(2,1)} %vir.1, f32[1,1024]{1,0:T(1,128)} %bitcast.14, f32[1,512]{1,0:T(1,128)} %bitcast.15, f32[32,1024]{1,0:T(8,128)} %constant.4.clone.ctab, f32[256,256]{1,0:T(8,128)} %constant.5.clone.btab), custom_call_target="tpu_custom_call" | custom-call | tf_op jit(solution)/shard_map/pallas_call | solution.py:432
  60.0 0.0 copy-start
  60.0 1.9 %copy.12 = f32[32,4,1024]{2,1,0:T(4,128)} copy(f32[32,4,1024]{2,1,0:T(4,128)} %bitcast.13) | data formatting | bytes 1048576
  62.0 0.0 copy-done
  62.0 0.8 %copy.13 = f32[32,4,1024]{2,1,0:T(4,128)} copy(f32[32,4,1024]{2,1,0:T(4,128)S(1)} %bitcast.12) | data formatting | bytes 1048576
Async XLA Ops:
  60.0 1.9 %copy-start = (f32[1024,128]{1,0:T(8,128)S(1)}, f32[1024,128]{1,0:T(8,128)}, u32[]{:S(2)}) copy-start(f32[1024,128]{1,0:T(8,128)} %get-tuple-element.5) | copy-start | bytes 1572868

commit v2 on v1

--- a/solution.py
+++ b/solution.py
@@ -87,7 +87,7 @@
     occ, vir, docc, dvir, ctab, btab, out_re, out_im,
     inb, dov, dvv, ctv, btv, mhi, mlo, nhi, nlo,
     pz, pb, rs, ra, rb, rc, yb, xr, zb,
-    in_sem, p1s, p1r, p2s, p2r, p3s, p3r, ras, rar, rbs, rbr, rcs, rcr, ys, yr,
+    in_sem, p1s, p1r, p2s, p2r, p3s, p3r, ras, rar, rbs, rbr, rcs, rcr, ys, yr, ready,
 ):
     row, col = lax.axis_index("row"), lax.axis_index("col")
     core = lax.rem(row, 2)
@@ -112,20 +112,22 @@
 
     barrier = pltpu.get_barrier_semaphore()
 
-    def greet(i, c):
+    def greet_z(i, c):
+        pl.semaphore_signal(barrier, inc=1, device_id=(row_of(xh, i, core), col), device_id_type=MESH)
+        return c
+
+    def greet_slab(i, c):
         pl.semaphore_signal(
-            barrier, inc=1, device_id=(xh * 16 + lax.div(i, 8), lax.rem(i, 8)), device_id_type=MESH
+            barrier, inc=1, device_id=(row_of(xh, z, lax.rem(i, 2)), lax.div(i, 2)), device_id_type=MESH
         )
         return c
 
-    lax.fori_loop(0, 128, greet, 0)
-
     def greet_other(i, c):
-        pl.semaphore_signal(
-            barrier, inc=1, device_id=(row_of(1 - xh, z, core), i), device_id_type=MESH
-        )
+        pl.semaphore_signal(barrier, inc=1, device_id=(row_of(1 - xh, z, core), i), device_id_type=MESH)
         return c
 
+    lax.fori_loop(0, 8, greet_z, 0)
+    lax.fori_loop(0, 16, greet_slab, 0)
     lax.fori_loop(0, 8, greet_other, 0)
 
     for load in loads:
@@ -142,7 +144,15 @@
         dec = jnp.sum(jnp.where(lane == band + 16 * row, dvv[...], 0.0), axis=1, keepdims=True)
         rs[32:48, :] = (inb[32:48, 0:1024].astype(F32) * dec).astype(BF16)
 
-    pl.semaphore_wait(barrier, 136)
+    pl.semaphore_wait(barrier, 32)
+
+    def greet_ready(i, c):
+        pl.semaphore_signal(
+            ready, inc=1, device_id=(row_of(xh, z, lax.rem(i, 2)), lax.div(i, 2)), device_id_type=MESH
+        )
+        return c
+
+    lax.fori_loop(0, 16, greet_ready, 0)
 
     def a_copy(s, c):
         lanes = pl.ds(pl.multiple_of(512 * s + 128 * lax.rem(c, 4), 128), 128)
@@ -344,6 +354,7 @@
 
         return carry
 
+    pl.semaphore_wait(ready, 16)
     lax.fori_loop(0, 64, y_send, 0)
 
     @pl.when(has_self)
@@ -461,6 +472,7 @@
             dma((8,)), dma((8,)),
             dma((4, 8)), dma((2, 2, 8)),
             dma, dma,
+            pltpu.SemaphoreType.REGULAR,
         ],
         compiler_params=pltpu.CompilerParams(collective_id=0, has_side_effects=True),
     )(

time: 62.9 us -> 59.5 us (0.946); the launches traced: 62.8 us -> 58.5 us
  Pallas kernels: 59.4 us -> 55.2 us
    pallas_call x1, Pallas kernels: 59.4 us -> 55.2 us  [on_device(): pl.pallas_call(kernel, out_shape=(out, out), in_specs=[anyspace] * 6, out...]
where the time goes in v2:
time: 59.5 us; the launch traced here: 58.5 us
  Pallas kernels  55.2 us (93%)
  local copies, waits for them, and re-layouts  2.72 us (5%)
  between operations  0.65 us (1%)
    pallas_call x1, Pallas kernels, on_device(): pl.pallas_call(kernel, out_shape=(out, out), in_specs=[anyspace] * 6, out...  55.2 us
    unnamed x4, local copies, waits for them, and re-layouts  2.72 us

profile of v2, /device:TPU:1, one launch (start us, length us, event | category | flops | bytes accessed | tf_op | source)
XLA Modules:
  0.0 58.5 jit_solution(11454494694040323215)
XLA Ops:
  0.6 55.2 %shard_map.77 = (f32[1024,128]{1,0:T(8,128)}, f32[1024,128]{1,0:T(8,128)}) custom-call(bf16[32,4096]{1,0:T(8,128)(2,1)} %occ.1, bf16[16,4096]{1,0:T(8,128)(2,1)} %vir.1, f32[1,1024]{1,0:T(1,128)} %bitcast.14, f32[1,512]{1,0:T(1,128)} %bitcast.15, f32[32,1024]{1,0:T(8,128)} %constant.4.clone.ctab, f32[256,256]{1,0:T(8,128)} %constant.5.clone.btab), custom_call_target="tpu_custom_call" | custom-call | tf_op jit(solution)/shard_map/pallas_call | solution.py:443
  55.8 0.0 copy-start
  55.8 1.9 %copy.12 = f32[32,4,1024]{2,1,0:T(4,128)} copy(f32[32,4,1024]{2,1,0:T(4,128)} %bitcast.13) | data formatting | bytes 1048576
  57.7 0.0 copy-done
  57.8 0.8 %copy.13 = f32[32,4,1024]{2,1,0:T(4,128)} copy(f32[32,4,1024]{2,1,0:T(4,128)S(1)} %bitcast.12) | data formatting | bytes 1048576
Async XLA Ops:
  55.8 1.9 %copy-start = (f32[1024,128]{1,0:T(8,128)S(1)}, f32[1024,128]{1,0:T(8,128)}, u32[]{:S(2)}) copy-start(f32[1024,128]{1,0:T(8,128)} %get-tuple-element.5) | copy-start | bytes 1572868

commit v3 on v2

--- a/solution.py
+++ b/solution.py
@@ -13,7 +13,8 @@
 F32 = jnp.float32
 BF16 = jnp.bfloat16
 SCALE = -(2.0**-17)
-DIST = (1, 7, 2, 6, 3, 5, 4)
+NEAR, FAR = (1, 7, 2, 6), (3, 5, 4)
+DIST = NEAR + FAR
 
 
 def angle_table(length):
@@ -231,7 +232,7 @@
         lax.fori_loop(0, 16, send, 0)
         ra[xh] = rs[:, pl.ds(pl.multiple_of(512 * xh, 512), 128)]
 
-    for dz in DIST[:2]:
+    for dz in NEAR:
         p1_copy(dz).start()
 
     mine = pl.ds(pl.multiple_of(z * 512, 512), 512)
@@ -245,7 +246,7 @@
 
     for dz in DIST:
         b_copy(dz).start()
-    for dz in DIST[2:]:
+    for dz in FAR:
         p1_copy(dz).start()
 
     blane = lax.rem(lax.div(lax.broadcasted_iota(jnp.int32, (32, 1024), 1), 4), 16)
@@ -283,27 +284,32 @@
 
     c_sends(z)
 
-    def step(i, carry):
-        dz = lax.rem(i, 2) * lax.div(i + 1, 2) + (1 - lax.rem(i, 2)) * (8 - lax.div(i, 2))
-        zs = lax.rem(z + 8 - dz, 8)
+    def source(dz):
+        return lax.rem(z + 8 - dz, 8)
+
+    def relay(dz):
+        zs = source(dz)
         p1_wait(zs)
         p2_copy(pz.at[zs], zs, 0).start()
         p2_copy(pz.at[zs], zs, 1).start()
-        b_wait(zs)
-        c_sends(zs)
-        return carry
-
-    lax.fori_loop(1, 8, step, 0)
-
-    def forward(i, carry):
-        dz = lax.rem(i, 2) * lax.div(i + 1, 2) + (1 - lax.rem(i, 2)) * lax.rem(8 - lax.div(i, 2), 8)
-        zs = lax.rem(z + 8 - dz, 8)
+
+    def forward(dz):
+        zs = source(dz)
         for xs in range(2):
             p2_wait(xs, zs)
             p3_copy(xs, zs).start()
-        return carry
-
-    lax.fori_loop(0, 8, forward, 0)
+
+    for dz in NEAR:
+        relay(dz)
+    for dz in DIST:
+        b_wait(source(dz))
+        c_sends(source(dz))
+    for dz in (0, *NEAR):
+        forward(dz)
+    for dz in FAR:
+        relay(dz)
+    for dz in FAR:
+        forward(dz)
 
     def arrive(zs, carry):
         for xs in range(2):
@@ -317,6 +323,18 @@
 
     lax.fori_loop(0, 8, arrive, 0)
 
+    slot = ((1 - xl) * 4 + y) * 8 + z
+    has_self = lax.div(z, 4) == core
+
+    def y_copy(m, c):
+        rows = pl.ds(pl.multiple_of(m * 32, 32), 32)
+        lanes = pl.ds(pl.multiple_of(c * 128, 128), 128)
+        return pltpu.make_async_remote_copy(
+            src_ref=yb.at[rows, lanes], dst_ref=xr.at[slot], send_sem=ys, recv_sem=yr,
+            device_id=(16 * xh + 8 * core + m, c), device_id_type=MESH,
+        )
+
+    pl.semaphore_wait(ready, 16)
     for yp in range(2):
         acc_o = jnp.zeros((128, 512), F32)
         acc_v = jnp.zeros((128, 512), F32)
@@ -333,29 +351,17 @@
         lo = (polar - hi.astype(F32)).astype(BF16)
         yb[128 * yp : 128 * yp + 128, :] = (mdot(hi, mhi[...]) + mdot(hi, mlo[...]) + mdot(lo, mhi[...])).astype(BF16)
 
-    slot = ((1 - xl) * 4 + y) * 8 + z
-    has_self = lax.div(z, 4) == core
-
-    def y_copy(m, c):
-        rows = pl.ds(pl.multiple_of(m * 32, 32), 32)
-        lanes = pl.ds(pl.multiple_of(c * 128, 128), 128)
-        return pltpu.make_async_remote_copy(
-            src_ref=yb.at[rows, lanes], dst_ref=xr.at[slot], send_sem=ys, recv_sem=yr,
-            device_id=(16 * xh + 8 * core + m, c), device_id_type=MESH,
-        )
-
-    def y_send(i, carry):
-        m = lax.rem(lax.div(i, 8) + 2 * z, 8)
-        c = lax.rem(lax.rem(i, 8) + col, 8)
-
-        @pl.when(jnp.logical_or(16 * xh + 8 * core + m != row, c != col))
-        def _():
-            y_copy(m, c).start()
-
-        return carry
-
-    pl.semaphore_wait(ready, 16)
-    lax.fori_loop(0, 64, y_send, 0)
+        def y_send(i, carry):
+            m = 4 * yp + lax.rem(i, 4)
+            c = lax.rem(lax.div(i, 4) + col, 8)
+
+            @pl.when(jnp.logical_or(16 * xh + 8 * core + m != row, c != col))
+            def _():
+                y_copy(m, c).start()
+
+            return carry
+
+        lax.fori_loop(0, 32, y_send, 0)
 
     @pl.when(has_self)
     def _():

time: 59.5 us -> 56.8 us (0.955); the launches traced: 58.5 us -> 56.7 us
  Pallas kernels: 55.2 us -> 53.3 us
    pallas_call x1, Pallas kernels: 55.2 us -> 53.3 us  [on_device(): pl.pallas_call(kernel, out_shape=(out, out), in_specs=[anyspace] * 6, out...]
where the time goes in v3:
time: 56.8 us; the launch traced here: 56.7 us
  Pallas kernels  53.3 us (94%)
  local copies, waits for them, and re-layouts  2.72 us (5%)
  between operations  0.65 us (1%)
    pallas_call x1, Pallas kernels, on_device(): pl.pallas_call(kernel, out_shape=(out, out), in_specs=[anyspace] * 6, out...  53.3 us
    unnamed x4, local copies, waits for them, and re-layouts  2.72 us

profile of v3, /device:TPU:1, one launch (start us, length us, event | category | flops | bytes accessed | tf_op | source)
XLA Modules:
  0.0 56.7 jit_solution(13439346175678880345)
XLA Ops:
  0.6 53.3 %shard_map.77 = (f32[1024,128]{1,0:T(8,128)}, f32[1024,128]{1,0:T(8,128)}) custom-call(bf16[32,4096]{1,0:T(8,128)(2,1)} %occ.1, bf16[16,4096]{1,0:T(8,128)(2,1)} %vir.1, f32[1,1024]{1,0:T(1,128)} %bitcast.14, f32[1,512]{1,0:T(1,128)} %bitcast.15, f32[32,1024]{1,0:T(8,128)} %constant.4.clone.ctab, f32[256,256]{1,0:T(8,128)} %constant.5.clone.btab), custom_call_target="tpu_custom_call" | custom-call | tf_op jit(solution)/shard_map/pallas_call | solution.py:449
  53.9 0.0 copy-start
  53.9 1.9 %copy.12 = f32[32,4,1024]{2,1,0:T(4,128)} copy(f32[32,4,1024]{2,1,0:T(4,128)} %bitcast.13) | data formatting | bytes 1048576
  55.9 0.0 copy-done
  55.9 0.8 %copy.13 = f32[32,4,1024]{2,1,0:T(4,128)} copy(f32[32,4,1024]{2,1,0:T(4,128)S(1)} %bitcast.12) | data formatting | bytes 1048576
Async XLA Ops:
  53.9 1.9 %copy-start = (f32[1024,128]{1,0:T(8,128)S(1)}, f32[1024,128]{1,0:T(8,128)}, u32[]{:S(2)}) copy-start(f32[1024,128]{1,0:T(8,128)} %get-tuple-element.5) | copy-start | bytes 1572868

commit v4 on v3

v4 whole, which is shorter than its diff:
```python
import functools
import math

import jax
import jax.numpy as jnp
import numpy as np
from jax import lax
from jax.experimental import pallas as pl
from jax.experimental.pallas import tpu as pltpu
from jax.sharding import PartitionSpec as P

MESH = pl.DeviceIdType.MESH
F32 = jnp.float32
BF16 = jnp.bfloat16
SCALE = -(2.0**-17)
NEAR, FAR = (1, 7, 2, 6), (3, 5, 4)
DIST = NEAR + FAR


def angle_table(length):
    k = np.arange(length)
    phase = np.outer(k, k) % length
    angle = 2.0 * np.pi * phase / length
    return np.cos(angle), np.sin(angle)


def c_table():
    cos, sin = angle_table(32)
    cos, sin = cos.reshape(32, 8, 1, 4), -sin.reshape(32, 8, 1, 4)
    both = np.stack([cos, sin], axis=2)
    return np.broadcast_to(both, (32, 8, 2, 16, 4)).reshape(32, 1024).astype(np.float32)


def b_table():
    cos, sin = angle_table(32)
    table = np.zeros((2, 2, 16, 4, 2, 4, 32), np.float32)
    for kc in range(4):
        c = cos.reshape(2, 16, 32)
        s = sin.reshape(2, 16, 32)
        table[:, 0, :, kc, 0, kc, :] = c
        table[:, 0, :, kc, 1, kc, :] = -s
        table[:, 1, :, kc, 0, kc, :] = s
        table[:, 1, :, kc, 1, kc, :] = c
    return table.reshape(256, 256)


def fft(parts):
    n = len(parts)
    if n == 1:
        return parts
    half = n // 2
    even, odd = fft(parts[0::2]), fft(parts[1::2])
    low, high = [], []
    for k in range(half):
        (ar, ai), (br, bi) = even[k], odd[k]
        if k == 0:
            tr, ti = br, bi
        elif 4 * k == n:
            tr, ti = bi, -br
        else:
            c, s = math.cos(2 * math.pi * k / n), math.sin(2 * math.pi * k / n)
            tr, ti = c * br + s * bi, c * bi - s * br
        low.append((ar + tr, ai + ti))
        high.append((ar - tr, ai - ti))
    return low + high


def swap_groups(v, lane):
    v = list(v)
    for shift, pairs in ((64, ((0, 2), (1, 3))), (32, ((0, 1), (2, 3)))):
        low = lax.rem(lane, 2 * shift) < shift
        for i, j in pairs:
            a, b = v[i], v[j]
            v[i] = jnp.where(low, a, pltpu.roll(b, shift, 1))
            v[j] = jnp.where(low, pltpu.roll(a, 128 - shift, 1), b)
    return v


def tdot(a, b):
    return lax.dot_general(a, b, (((0,), (0,)), ((), ())), preferred_element_type=F32)


def mdot(a, b):
    return jnp.dot(a, b, preferred_element_type=F32)


def kernel(
    occ, vir, docc, dvir, ctab, xr,
    inb, dov, dvv, ctv, mhi, mlo,
    pz, pb, rs, rc, yb,
    in_sem, p1s, p1r, p2s, p2r, p3s, p3r, ras, rar, rbs, rbr, rcs, rcr, ys, yr, ready,
):
    row, col = lax.axis_index("row"), lax.axis_index("col")
    core = lax.rem(row, 2)
    z = lax.rem(lax.div(row, 2), 8)
    xh = lax.div(row, 16)
    y, xl = lax.rem(col, 4), lax.div(col, 4)
    x = 2 * xh + xl

    def row_of(xh_, z_, k_):
        return (xh_ * 8 + z_) * 2 + k_

    loads = [
        pltpu.make_async_copy(occ, inb.at[pl.ds(0, 32)], in_sem.at[0]),
        pltpu.make_async_copy(vir, inb.at[pl.ds(32, 16)], in_sem.at[1]),
        pltpu.make_async_copy(docc, dov, in_sem.at[2]),
        pltpu.make_async_copy(dvir, dvv, in_sem.at[3]),
        pltpu.make_async_copy(ctab, ctv, in_sem.at[4]),
    ]
    for load in loads:
        load.start()

    barrier = pltpu.get_barrier_semaphore()

    def greet_z(i, c):
        pl.semaphore_signal(barrier, inc=1, device_id=(row_of(xh, i, core), col), device_id_type=MESH)
        return c

    def greet_slab(i, c):
        pl.semaphore_signal(
            barrier, inc=1, device_id=(row_of(xh, z, lax.rem(i, 2)), lax.div(i, 2)), device_id_type=MESH
        )
        return c

    def greet_other(i, c):
        pl.semaphore_signal(
            barrier, inc=1, device_id=(row_of(1 - xh, z, lax.rem(i, 2)), lax.div(i, 2)), device_id_type=MESH
        )
        return c

    lax.fori_loop(0, 8, greet_z, 0)
    lax.fori_loop(0, 16, greet_slab, 0)
    lax.fori_loop(0, 16, greet_other, 0)

    for load in loads:
        load.wait()

    @pl.when(col == 0)
    def _():
        lane = lax.broadcasted_iota(jnp.int32, (32, 1024), 1)
        band = lax.broadcasted_iota(jnp.int32, (32, 1024), 0)
        dec = jnp.sum(jnp.where(lane == band + 32 * row, dov[...], 0.0), axis=1, keepdims=True)
        rs[0:32, :] = (inb[0:32, 0:1024].astype(F32) * dec).astype(BF16)
        lane = lax.broadcasted_iota(jnp.int32, (16, 512), 1)
        band = lax.broadcasted_iota(jnp.int32, (16, 512), 0)
        dec = jnp.sum(jnp.where(lane == band + 16 * row, dvv[...], 0.0), axis=1, keepdims=True)
        rs[32:48, :] = (inb[32:48, 0:1024].astype(F32) * dec).astype(BF16)

    pl.semaphore_wait(barrier, 40)

    def greet_ready(i, c):
        pl.semaphore_signal(
            ready, inc=1, device_id=(row_of(xh, z, lax.rem(i, 2)), lax.div(i, 2)), device_id_type=MESH
        )
        return c

    lax.fori_loop(0, 16, greet_ready, 0)

    def half(h):
        return pl.ds(128 * h, 128)

    def a_copy(h, i):
        s, kk, xt = lax.div(i, 4), lax.rem(lax.div(i, 2), 2), lax.rem(i, 2)
        lanes = pl.ds(pl.multiple_of(512 * s + 256 * kk + 128 * h, 128), 128)
        b = 2 * xh + core
        return pltpu.make_async_remote_copy(
            src_ref=rs.at[:, lanes], dst_ref=rc.at[b, z, :, half(h)], send_sem=ras.at[h, i], recv_sem=rar.at[h],
            device_id=(row_of(s, z, kk), xt * 4 + b), device_id_type=MESH,
        )

    def a_wait(h):
        ref = rc.at[y, z, :, half(h)]
        pltpu.make_async_copy(ref, ref, rar.at[h]).wait()

    def b_copy(h, dz):
        ref = rc.at[y, z, :, half(h)]
        return pltpu.make_async_remote_copy(
            src_ref=ref, dst_ref=ref, send_sem=rbs.at[h, dz], recv_sem=rbr.at[h, z],
            device_id=(row_of(xh, lax.rem(z + dz, 8), core), col), device_id_type=MESH,
        )

    def b_wait(h, zs):
        ref = rc.at[y, zs, :, half(h)]
        pltpu.make_async_copy(ref, ref, rbr.at[h, zs]).wait()

    def c_copy(h, zs, dy):
        ref = rc.at[y, zs, :, half(h)]
        return pltpu.make_async_remote_copy(
            src_ref=ref, dst_ref=ref, send_sem=rcs.at[h, dy, zs], recv_sem=rcr.at[h, y, zs],
            device_id=(row, xl * 4 + lax.rem(y + dy, 4)), device_id_type=MESH,
        )

    def c_wait(h, b, zs):
        ref = rc.at[b, zs, :, half(h)]
        pltpu.make_async_copy(ref, ref, rcr.at[h, b, zs]).wait()

    def p1_copy(dz):
        zt = lax.rem(z + dz, 8)
        lanes = pl.ds(pl.multiple_of(zt * 512, 512), 512)
        return pltpu.make_async_remote_copy(
            src_ref=inb.at[:, lanes], dst_ref=pz.at[z], send_sem=p1s.at[dz], recv_sem=p1r.at[z],
            device_id=(row_of(xh, zt, core), col), device_id_type=MESH,
        )

    def p1_wait(zs):
        pltpu.make_async_copy(pz.at[zs], pz.at[zs], p1r.at[zs]).wait()

    def p2_copy(src, zs, side):
        xt = lax.rem(x + 1 + 2 * side, 4)
        return pltpu.make_async_remote_copy(
            src_ref=src, dst_ref=pb.at[2 * xh + core, zs], send_sem=p2s.at[side, zs], recv_sem=p2r.at[xh, zs],
            device_id=(row_of(lax.div(xt, 2), z, core), lax.rem(xt, 2) * 4 + y), device_id_type=MESH,
        )

    def p2_wait(xs, zs):
        pltpu.make_async_copy(pb.at[2 * xs + core, zs], pb.at[2 * xs + core, zs], p2r.at[xs, zs]).wait()

    def p3_copy(xs, zs):
        return pltpu.make_async_remote_copy(
            src_ref=pb.at[2 * xs + core, zs], dst_ref=pb.at[2 * xs + core, zs], send_sem=p3s.at[xs, zs],
            recv_sem=p3r.at[xs, zs], device_id=(row + 1 - 2 * core, col), device_id_type=MESH,
        )

    def p3_wait(xs, zs):
        other = 1 - core
        pltpu.make_async_copy(pb.at[2 * xs + other, zs], pb.at[2 * xs + other, zs], p3r.at[xs, zs]).wait()

    self_a = jnp.logical_and(col == 0, jnp.logical_and(xh == 0, core == 0))

    @pl.when(col == 0)
    def _():
        def send(i, carry):
            @pl.when(jnp.logical_or(lax.rem(i, 8) != 0, jnp.logical_not(self_a)))
            def _():
                a_copy(lax.div(i, 8), lax.rem(i, 8)).start()

            return carry

        lax.fori_loop(0, 16, send, 0)

    @pl.when(self_a)
    def _():
        rc[0, z] = rs[:, 0:256]

    def near_y(h, zs):
        for dy in (1, 3, 2):
            c_copy(h, zs, dy).start()

    def scattered(h):
        @pl.when(jnp.logical_not(self_a))
        def _():
            a_wait(h)

        for dz in DIST:
            b_copy(h, dz).start()
        near_y(h, z)

    for dz in NEAR:
        p1_copy(dz).start()

    mine = pl.ds(pl.multiple_of(z * 512, 512), 512)
    for side in range(2):
        p2_copy(inb.at[:, mine], z, side).start()

    scattered(0)
    for dz in FAR:
        p1_copy(dz).start()
    scattered(1)

    blane = lax.rem(lax.div(lax.broadcasted_iota(jnp.int32, (32, 1024), 1), 4), 16)
    ct = ctv[...]
    ct_hi = ct.astype(BF16).astype(F32)
    ct_lo = ct - ct_hi

    def table(b, c):
        rows = pl.ds(pl.multiple_of(b * 32, 32), 32)
        mhi[rows, :] = jnp.where(blane == b, ct_hi, 0.0).astype(BF16)
        mlo[rows, :] = jnp.where(blane == b, ct_lo, 0.0).astype(BF16)
        return c

    lax.fori_loop(0, 16, table, 0)
    def source(dz):
        return lax.rem(z + 8 - dz, 8)

    def relay(dz):
        zs = source(dz)
        p1_wait(zs)
        p2_copy(pz.at[zs], zs, 0).start()
        p2_copy(pz.at[zs], zs, 1).start()

    def forward(dz):
        zs = source(dz)
        for xs in range(2):
            p2_wait(xs, zs)
            p3_copy(xs, zs).start()

    for dz in NEAR:
        relay(dz)
    for dz in DIST:
        b_wait(0, source(dz))
        near_y(0, source(dz))
    for dz in (0, *NEAR):
        forward(dz)
    for dz in FAR:
        relay(dz)
    for dz in DIST:
        b_wait(1, source(dz))
        near_y(1, source(dz))
    for dz in FAR:
        forward(dz)

    def arrive(zs, carry):
        for xs in range(2):
            p3_wait(xs, zs)
        return carry

    lax.fori_loop(0, 8, arrive, 0)

    slot = ((1 - xl) * 4 + y) * 8 + z
    has_self = lax.div(z, 4) == core

    def y_copy(m, c):
        rows = pl.ds(pl.multiple_of(m * 32, 32), 32)
        lanes = pl.ds(pl.multiple_of(c * 128, 128), 128)
        return pltpu.make_async_remote_copy(
            src_ref=yb.at[rows, lanes], dst_ref=xr.at[slot], send_sem=ys, recv_sem=yr,
            device_id=(16 * xh + 8 * core + m, c), device_id_type=MESH,
        )

    pl.semaphore_wait(ready, 16)
    for h in range(2):
        def gathered(zs, carry):
            for dy in range(1, 4):
                c_wait(h, lax.rem(y + dy, 4), zs)
            return carry

        lax.fori_loop(0, 8, gathered, 0)

        acc_o = jnp.zeros((128, 512), F32)
        acc_v = jnp.zeros((128, 512), F32)
        lanes = slice(128 * h, 128 * h + 128)
        for b in range(4):
            acc_o += tdot(rc[b, :, 0:32, lanes].reshape(256, 128), pb[b, :, 0:32, :].reshape(256, 512))
            acc_v += tdot(rc[b, :, 32:48, lanes].reshape(128, 128), pb[b, :, 32:48, :].reshape(128, 512))
        polar = acc_o * acc_v * SCALE
        hi = polar.astype(BF16)
        lo = (polar - hi.astype(F32)).astype(BF16)
        yb[128 * h : 128 * h + 128, :] = (mdot(hi, mhi[...]) + mdot(hi, mlo[...]) + mdot(lo, mhi[...])).astype(BF16)

        def y_send(i, carry):
            m = 4 * h + lax.rem(i, 4)
            c = lax.rem(lax.div(i, 4) + col, 8)

            @pl.when(jnp.logical_or(16 * xh + 8 * core + m != row, c != col))
            def _():
                y_copy(m, c).start()

            return carry

        lax.fori_loop(0, 32, y_send, 0)

    @pl.when(has_self)
    def _():
        m = row - 16 * xh - 8 * core
        xr[slot] = yb[pl.ds(pl.multiple_of(m * 32, 32), 32), pl.ds(pl.multiple_of(col * 128, 128), 128)]
        pltpu.make_async_copy(xr.at[pl.ds(0, 63)], xr.at[pl.ds(0, 63)], yr).wait()

    @pl.when(jnp.logical_not(has_self))
    def _():
        pltpu.make_async_copy(xr, xr, yr).wait()

    @pl.when(col == 0)
    def _():
        def sent(i, carry):
            @pl.when(jnp.logical_or(lax.rem(i, 8) != 0, jnp.logical_not(self_a)))
            def _():
                a_copy(lax.div(i, 8), lax.rem(i, 8)).wait_send()

            return carry

        lax.fori_loop(0, 16, sent, 0)

    def sent_z(dz, carry):
        p1_copy(dz).wait_send()
        for h in range(2):
            b_copy(h, dz).wait_send()
        return carry

    lax.fori_loop(1, 8, sent_z, 0)

    def sent_zs(zs, carry):
        for side in range(2):
            p2_copy(pz.at[zs], zs, side).wait_send()
            p3_copy(side, zs).wait_send()
        for h in range(2):
            for dy in range(1, 4):
                c_copy(h, zs, dy).wait_send()
        return carry

    lax.fori_loop(0, 8, sent_zs, 0)

    @pl.when(has_self)
    def _():
        pltpu.make_async_copy(xr.at[pl.ds(0, 63)], xr.at[pl.ds(0, 63)], ys).wait()

    @pl.when(jnp.logical_not(has_self))
    def _():
        pltpu.make_async_copy(xr, xr, ys).wait()


def finish(xr, btab, out_re, out_im, nhi, nlo, zb, res_re, res_im, sem):
    bt = btab[...]
    bt_hi = bt.astype(BF16)
    nhi[...] = bt_hi
    nlo[...] = (bt - bt_hi.astype(F32)).astype(BF16)

    def b_step(i, carry):
        part = xr[pl.ds(pl.multiple_of(16 * i, 16), 16)].reshape(8, 2, 32, 128)
        both = jnp.concatenate([part[:, 0].reshape(256, 128), part[:, 1].reshape(256, 128)], axis=1)
        res = mdot(both, nhi[...]) + mdot(both, nlo[...])
        zb[pl.ds(8 * i, 8)] = res.reshape(8, 32, 256)
        return carry

    lax.fori_loop(0, 4, b_step, 0)

    lane = lax.broadcasted_iota(jnp.int32, (8, 128), 1)

    def put(i, which):
        res, out = ((res_re, out_re), (res_im, out_im))[which]
        rows = pl.ds(pl.multiple_of(256 * i, 256), 256)
        return pltpu.make_async_copy(res.at[rows], out.at[rows], sem.at[which, i])

    def a_step(i, carry):
        rows = pl.ds(pl.multiple_of(8 * i, 8), 8)
        res = fft([(zb[a, rows, 0:128], zb[a, rows, 128:256]) for a in range(32)])
        for j in range(8):
            for part, out in ((0, res_re), (1, res_im)):
                moved = swap_groups([res[4 * j + t][part] for t in range(4)], lane)
                for kc in range(4):
                    out[pl.ds(i * 256 + j * 4 + kc, 8, stride=32), :] = moved[kc]
        put(i, 0).start()
        put(i, 1).start()
        return carry

    lax.fori_loop(0, 4, a_step, 0)
    for i in range(4):
        put(i, 0).wait()
        put(i, 1).wait()


def on_device(occ, vir, docc, dvir):
    anyspace = pl.BlockSpec(memory_space=pl.ANY)
    vmem = pl.BlockSpec(memory_space=pltpu.VMEM)
    dma = pltpu.SemaphoreType.DMA
    xr = pl.pallas_call(
        kernel,
        out_shape=pltpu.VMEM((64, 32, 128), BF16),
        in_specs=[anyspace] * 5,
        out_specs=vmem,
        scratch_shapes=[
            pltpu.VMEM((48, 4096), BF16),
            pltpu.VMEM((1, 1024), F32),
            pltpu.VMEM((1, 512), F32),
            pltpu.VMEM((32, 1024), F32),
            pltpu.VMEM((512, 1024), BF16),
            pltpu.VMEM((512, 1024), BF16),
            pltpu.VMEM((8, 48, 512), BF16),
            pltpu.VMEM((4, 8, 48, 512), BF16),
            pltpu.VMEM((48, 1024), BF16),
            pltpu.VMEM((4, 8, 48, 256), BF16),
            pltpu.VMEM((256, 1024), BF16),
            dma((5,)),
            dma((8,)), dma((8,)),
            dma((2, 8)), dma((2, 8)),
            dma((2, 8)), dma((2, 8)),
            dma((2, 8)), dma((2,)),
            dma((2, 8)), dma((2, 8)),
            dma((2, 4, 8)), dma((2, 4, 8)),
            dma, dma,
            pltpu.SemaphoreType.REGULAR,
        ],
        compiler_params=pltpu.CompilerParams(collective_id=0, has_side_effects=True),
    )(occ, vir, docc.reshape(1, 1024), dvir.reshape(1, 512), jnp.asarray(c_table()))
    out = jax.ShapeDtypeStruct((1024, 128), F32)
    res = pl.pallas_call(
        finish,
        out_shape=(out, out),
        in_specs=[vmem, vmem],
        out_specs=(anyspace, anyspace),
        scratch_shapes=[
            pltpu.VMEM((256, 256), BF16),
            pltpu.VMEM((256, 256), BF16),
            pltpu.VMEM((32, 32, 256), F32),
            pltpu.VMEM((1024, 128), F32),
            pltpu.VMEM((1024, 128), F32),
            dma((2, 4)),
        ],
    )(pltpu.with_memory_space_constraint(xr, pltpu.VMEM), jnp.asarray(b_table()))

    def placed(part):
        return jnp.transpose(part.reshape(32, 8, 4, 128), (0, 2, 1, 3)).reshape(32, 4, 1024)

    return placed(res[0]), placed(res[1])


def solution(mesh):
    in_specs = (P("row", "col"), P("row", "col"), P(), P())
    out_specs = (P("row", "col", None), P("row", "col", None))
    return jax.shard_map(
        on_device, mesh=mesh, in_specs=in_specs, out_specs=out_specs, check_vma=False
    )
```

time: 56.8 us -> 54 us (0.951)
  local copies, waits for them, and re-layouts: 2.72 us -> 0 us
    unnamed x4 -> x0, local copies, waits for them, and re-layouts: 2.72 us -> none
    pallas_call x1 -> x2, Pallas kernels: 53.3 us -> 53.2 us  [the longest x1 49.1 us: on_device(): pl.pallas_call(kernel, out_shape=pltpu.VMEM((64, 32, 128), BF16), in_spec...]
where the time goes in v4:
time: 54 us; the launch traced here: 53.8 us
  Pallas kernels  53.2 us (99%)
  between operations  0.64 us (1%)
    pallas_call x1, Pallas kernels, on_device(): pl.pallas_call(kernel, out_shape=pltpu.VMEM((64, 32, 128), BF16), in_spec...  49.1 us
    pallas_call x1, Pallas kernels, on_device(): pl.pallas_call(finish, out_shape=(out, out), in_specs=[vmem, vmem], out_s...  4.05 us

profile of v4, /device:TPU:1, one launch (start us, length us, event | category | flops | bytes accessed | tf_op | source)
XLA Modules:
  0.0 53.8 jit_solution(15859146370324172890)
XLA Ops:
  0.6 49.1 %shard_map.77.xr = bf16[64,32,128]{2,1,0:T(8,128)(2,1)S(1)} custom-call(bf16[32,4096]{1,0:T(8,128)(2,1)} %occ.1, bf16[16,4096]{1,0:T(8,128)(2,1)} %vir.1, f32[1,1024]{1,0:T(1,128)} %bitcast.12, f32[1,512]{1,0:T(1,128)} %bitcast.13, f32[32,1024]{1,0:T(8,128)} %constant.4.clone.ctab), custom_call_target="tpu_custom_call" | custom-call | tf_op jit(solution)/shard_map/pallas_call | solution.py:455
  49.8 4.0 %shard_map.78 = (f32[1024,128]{1,0:T(8,128)}, f32[1024,128]{1,0:T(8,128)}) custom-call(bf16[64,32,128]{2,1,0:T(8,128)(2,1)S(1)} %shard_map.77.xr, f32[256,256]{1,0:T(8,128)} %constant.5.clone.btab), custom_call_target="tpu_custom_call" | custom-call | tf_op jit(solution)/shard_map/pallas_call | solution.py:485

commit v5 on v4

v5 whole, which is shorter than its diff:
```python
import functools
import math

import jax
import jax.numpy as jnp
import numpy as np
from jax import lax
from jax.experimental import pallas as pl
from jax.experimental.pallas import tpu as pltpu
from jax.sharding import PartitionSpec as P

MESH = pl.DeviceIdType.MESH
F32 = jnp.float32
BF16 = jnp.bfloat16
SCALE = -(2.0**-17)
NEAR, FAR = (1, 7, 2, 6), (3, 5, 4)
DIST = NEAR + FAR


def angle_table(length):
    k = np.arange(length)
    phase = np.outer(k, k) % length
    angle = 2.0 * np.pi * phase / length
    return np.cos(angle), np.sin(angle)


def c_table():
    cos, sin = angle_table(32)
    cos, sin = cos.reshape(32, 8, 1, 4), -sin.reshape(32, 8, 1, 4)
    both = np.stack([cos, sin], axis=2)
    return np.broadcast_to(both, (32, 8, 2, 16, 4)).reshape(32, 1024).astype(np.float32)


def b_table():
    cos, sin = angle_table(32)
    table = np.zeros((2, 2, 16, 4, 2, 4, 32), np.float32)
    for kc in range(4):
        c = cos.reshape(2, 16, 32)
        s = sin.reshape(2, 16, 32)
        table[:, 0, :, kc, 0, kc, :] = c
        table[:, 0, :, kc, 1, kc, :] = -s
        table[:, 1, :, kc, 0, kc, :] = s
        table[:, 1, :, kc, 1, kc, :] = c
    return table.reshape(256, 256)


def fft(parts):
    n = len(parts)
    if n == 1:
        return parts
    half = n // 2
    even, odd = fft(parts[0::2]), fft(parts[1::2])
    low, high = [], []
    for k in range(half):
        (ar, ai), (br, bi) = even[k], odd[k]
        if k == 0:
            tr, ti = br, bi
        elif 4 * k == n:
            tr, ti = bi, -br
        else:
            c, s = math.cos(2 * math.pi * k / n), math.sin(2 * math.pi * k / n)
            tr, ti = c * br + s * bi, c * bi - s * br
        low.append((ar + tr, ai + ti))
        high.append((ar - tr, ai - ti))
    return low + high


def swap_groups(v, lane):
    v = list(v)
    for shift, pairs in ((64, ((0, 2), (1, 3))), (32, ((0, 1), (2, 3)))):
        low = lax.rem(lane, 2 * shift) < shift
        for i, j in pairs:
            a, b = v[i], v[j]
            v[i] = jnp.where(low, a, pltpu.roll(b, shift, 1))
            v[j] = jnp.where(low, pltpu.roll(a, 128 - shift, 1), b)
    return v


def tdot(a, b):
    return lax.dot_general(a, b, (((0,), (0,)), ((), ())), preferred_element_type=F32)


def mdot(a, b):
    return jnp.dot(a, b, preferred_element_type=F32)


def kernel(
    occ, vir, docc, dvir, ctab, btab, xr, ntab,
    inb, dov, dvv, ctv, mtab,
    pz, pb, rs, rc, yb,
    in_sem, p1s, p1r, p2s, p2r, p3s, p3r, ras, rar, rbs, rbr, rxs, rxr, rcs, rcr, ys, yr, ready,
):
    row, col = lax.axis_index("row"), lax.axis_index("col")
    core = lax.rem(row, 2)
    z = lax.rem(lax.div(row, 2), 8)
    xh = lax.div(row, 16)
    y, xl = lax.rem(col, 4), lax.div(col, 4)
    x = 2 * xh + xl

    def row_of(xh_, z_, k_):
        return (xh_ * 8 + z_) * 2 + k_

    loads = [
        pltpu.make_async_copy(occ, inb.at[pl.ds(0, 32)], in_sem.at[0]),
        pltpu.make_async_copy(vir, inb.at[pl.ds(32, 16)], in_sem.at[1]),
        pltpu.make_async_copy(docc, dov, in_sem.at[2]),
        pltpu.make_async_copy(dvir, dvv, in_sem.at[3]),
        pltpu.make_async_copy(ctab, ctv, in_sem.at[4]),
        pltpu.make_async_copy(btab, ntab, in_sem.at[5]),
    ]
    for load in loads:
        load.start()

    barrier = pltpu.get_barrier_semaphore()

    def greet_z(i, c):
        pl.semaphore_signal(barrier, inc=1, device_id=(row_of(xh, i, core), col), device_id_type=MESH)
        return c

    def greet_slab(i, c):
        pl.semaphore_signal(
            barrier, inc=1, device_id=(row_of(xh, z, lax.rem(i, 2)), lax.div(i, 2)), device_id_type=MESH
        )
        return c

    def greet_other(i, c):
        pl.semaphore_signal(
            barrier, inc=1, device_id=(row_of(1 - xh, z, lax.rem(i, 2)), lax.div(i, 2)), device_id_type=MESH
        )
        return c

    lax.fori_loop(0, 8, greet_z, 0)
    lax.fori_loop(0, 16, greet_slab, 0)
    lax.fori_loop(0, 16, greet_other, 0)

    for load in loads:
        load.wait()

    @pl.when(col == 0)
    def _():
        lane = lax.broadcasted_iota(jnp.int32, (32, 1024), 1)
        band = lax.broadcasted_iota(jnp.int32, (32, 1024), 0)
        dec = jnp.sum(jnp.where(lane == band + 32 * row, dov[...], 0.0), axis=1, keepdims=True)
        rs[0:32, :] = (inb[0:32, 0:1024].astype(F32) * dec).astype(BF16)
        lane = lax.broadcasted_iota(jnp.int32, (16, 512), 1)
        band = lax.broadcasted_iota(jnp.int32, (16, 512), 0)
        dec = jnp.sum(jnp.where(lane == band + 16 * row, dvv[...], 0.0), axis=1, keepdims=True)
        rs[32:48, :] = (inb[32:48, 0:1024].astype(F32) * dec).astype(BF16)

    pl.semaphore_wait(barrier, 40)

    def greet_ready(i, c):
        pl.semaphore_signal(
            ready, inc=1, device_id=(row_of(xh, z, lax.rem(i, 2)), lax.div(i, 2)), device_id_type=MESH
        )
        return c

    lax.fori_loop(0, 16, greet_ready, 0)

    def landed(ref, sem):
        pltpu.make_async_copy(ref, ref, sem).wait()

    def a_copy(i):
        s, kk, xt = lax.div(i, 4), lax.rem(lax.div(i, 2), 2), lax.rem(i, 2)
        lanes = pl.ds(pl.multiple_of(512 * s + 256 * kk + 128 * xt, 128), 128)
        b = 2 * xh + core
        return pltpu.make_async_remote_copy(
            src_ref=rs.at[:, lanes], dst_ref=rc.at[0, b, z], send_sem=ras, recv_sem=rar,
            device_id=(row_of(s, z, kk), xt * 4 + b), device_id_type=MESH,
        )

    def b_copy(dz):
        ref = rc.at[0, y, z]
        return pltpu.make_async_remote_copy(
            src_ref=ref, dst_ref=ref, send_sem=rbs, recv_sem=rbr.at[z],
            device_id=(row_of(xh, lax.rem(z + dz, 8), core), col), device_id_type=MESH,
        )

    def x_copy(zs):
        return pltpu.make_async_remote_copy(
            src_ref=rc.at[0, y, zs], dst_ref=rc.at[1, y, zs], send_sem=rxs, recv_sem=rxr.at[zs],
            device_id=(row, (1 - xl) * 4 + y), device_id_type=MESH,
        )

    def c_copy(o, zs, dy):
        ref = rc.at[o, y, zs]
        return pltpu.make_async_remote_copy(
            src_ref=ref, dst_ref=ref, send_sem=rcs, recv_sem=rcr.at[o],
            device_id=(row, xl * 4 + lax.rem(y + dy, 4)), device_id_type=MESH,
        )

    def near_y(o, zs):
        for dy in (1, 3, 2):
            c_copy(o, zs, dy).start()

    def p1_copy(dz):
        zt = lax.rem(z + dz, 8)
        lanes = pl.ds(pl.multiple_of(zt * 512, 512), 512)
        return pltpu.make_async_remote_copy(
            src_ref=inb.at[:, lanes], dst_ref=pz.at[z], send_sem=p1s, recv_sem=p1r.at[z],
            device_id=(row_of(xh, zt, core), col), device_id_type=MESH,
        )

    def p2_copy(src, zs, side):
        xt = lax.rem(x + 1 + 2 * side, 4)
        return pltpu.make_async_remote_copy(
            src_ref=src, dst_ref=pb.at[2 * xh + core, zs], send_sem=p2s, recv_sem=p2r.at[zs],
            device_id=(row_of(lax.div(xt, 2), z, core), lax.rem(xt, 2) * 4 + y), device_id_type=MESH,
        )

    def p3_copy(xs, zs):
        return pltpu.make_async_remote_copy(
            src_ref=pb.at[2 * xs + core, zs], dst_ref=pb.at[2 * xs + core, zs], send_sem=p3s,
            recv_sem=p3r, device_id=(row + 1 - 2 * core, col), device_id_type=MESH,
        )

    self_a = jnp.logical_and(col == 0, jnp.logical_and(xh == 0, core == 0))

    @pl.when(col == 0)
    def _():
        def send(i, carry):
            @pl.when(jnp.logical_or(i != 0, jnp.logical_not(self_a)))
            def _():
                a_copy(i).start()

            return carry

        lax.fori_loop(0, 8, send, 0)

    @pl.when(self_a)
    def _():
        rc[0, 0, z] = rs[:, 0:128]

    for dz in NEAR:
        p1_copy(dz).start()

    mine = pl.ds(pl.multiple_of(z * 512, 512), 512)
    for side in range(2):
        p2_copy(inb.at[:, mine], z, side).start()

    @pl.when(jnp.logical_not(self_a))
    def _():
        landed(rc.at[0, y, z], rar)

    for dz in DIST:
        b_copy(dz).start()
    near_y(0, z)
    x_copy(z).start()
    for dz in FAR:
        p1_copy(dz).start()

    blane = lax.rem(lax.div(lax.broadcasted_iota(jnp.int32, (32, 1024), 1), 4), 16)
    ct = ctv[...]

    def table(b, c):
        rows = pl.ds(pl.multiple_of(b * 32, 32), 32)
        mtab[rows, :] = jnp.where(blane == b, ct, 0.0).astype(BF16)
        return c

    lax.fori_loop(0, 16, table, 0)

    def source(dz):
        return lax.rem(z + 8 - dz, 8)

    def relay(dz):
        zs = source(dz)
        landed(pz.at[zs], p1r.at[zs])
        p2_copy(pz.at[zs], zs, 0).start()
        p2_copy(pz.at[zs], zs, 1).start()

    def forward(dz):
        zs = source(dz)
        landed(pb.at[pl.ds(0, 2), zs], p2r.at[zs])
        p3_copy(0, zs).start()
        p3_copy(1, zs).start()

    for dz in NEAR:
        relay(dz)
    for dz in DIST:
        zs = source(dz)
        landed(rc.at[0, y, zs], rbr.at[zs])
        near_y(0, zs)
        x_copy(zs).start()
    for dz in FAR:
        relay(dz)
    for dz in (0, *NEAR):
        forward(dz)
    for dz in (0, *DIST):
        zs = source(dz)
        landed(rc.at[1, y, zs], rxr.at[zs])
        near_y(1, zs)
    for dz in FAR:
        forward(dz)
    landed(pb.at[pl.ds(0, 2)], p3r)

    slot = ((1 - xl) * 4 + y) * 8 + z
    has_self = lax.div(z, 4) == core

    def y_copy(o, i, c):
        rows = pl.ds(pl.multiple_of(o * 128 + i * 32, 32), 32)
        lanes = pl.ds(pl.multiple_of(c * 128, 128), 128)
        return pltpu.make_async_remote_copy(
            src_ref=yb.at[rows, lanes], dst_ref=xr.at[slot], send_sem=ys, recv_sem=yr,
            device_id=(16 * xh + 8 * core + 4 * half(o) + i, c), device_id_type=MESH,
        )

    def half(o):
        return xl + o - 2 * xl * o

    pl.semaphore_wait(ready, 16)
    for o in range(2):
        landed(rc.at[o, pl.ds(0, 3)], rcr.at[o])
        acc_o = jnp.zeros((128, 512), F32)
        acc_v = jnp.zeros((128, 512), F32)
        for b in range(4):
            acc_o += tdot(rc[o, b, :, 0:32, :].reshape(256, 128), pb[b, :, 0:32, :].reshape(256, 512))
            acc_v += tdot(rc[o, b, :, 32:48, :].reshape(128, 128), pb[b, :, 32:48, :].reshape(128, 512))
        polar = (acc_o * acc_v * SCALE).astype(BF16)
        yb[128 * o : 128 * o + 128, :] = mdot(polar, mtab[...]).astype(BF16)

        def y_send(j, carry):
            i = lax.rem(j, 4)
            c = lax.rem(lax.div(j, 4) + col, 8)

            @pl.when(jnp.logical_or(16 * xh + 8 * core + 4 * half(o) + i != row, c != col))
            def _():
                y_copy(o, i, c).start()

            return carry

        lax.fori_loop(0, 32, y_send, 0)

    @pl.when(has_self)
    def _():
        m = row - 16 * xh - 8 * core
        o = jnp.abs(lax.div(m, 4) - xl)
        rows = pl.ds(pl.multiple_of(o * 128 + lax.rem(m, 4) * 32, 32), 32)
        xr[slot] = yb[rows, pl.ds(pl.multiple_of(col * 128, 128), 128)]
        landed(xr.at[pl.ds(0, 63)], yr)

    @pl.when(jnp.logical_not(has_self))
    def _():
        landed(xr, yr)

    @pl.when(jnp.logical_and(col == 0, jnp.logical_not(self_a)))
    def _():
        landed(rc.at[0, 0], ras)

    @pl.when(self_a)
    def _():
        landed(rc.at[0, 0, pl.ds(0, 7)], ras)

    landed(pz.at[pl.ds(0, 7)], p1s)
    landed(rc.at[0, 0, pl.ds(0, 7)], rbs)
    landed(rc.at[0, 0], rxs)
    landed(pb.at[pl.ds(0, 2)], p2s)
    landed(pb.at[pl.ds(0, 2)], p3s)
    landed(rc.at[0, pl.ds(0, 3)], rcs)
    landed(rc.at[1, pl.ds(0, 3)], rcs)

    @pl.when(has_self)
    def _():
        landed(xr.at[pl.ds(0, 63)], ys)

    @pl.when(jnp.logical_not(has_self))
    def _():
        landed(xr, ys)


def finish(xr, ntab, out_re, out_im, zb, res_re, res_im, sem):
    def b_step(i, carry):
        part = xr[pl.ds(pl.multiple_of(16 * i, 16), 16)].reshape(8, 2, 32, 128)
        both = jnp.concatenate([part[:, 0].reshape(256, 128), part[:, 1].reshape(256, 128)], axis=1)
        res = mdot(both, ntab[...])
        zb[pl.ds(8 * i, 8)] = res.reshape(8, 32, 256)
        return carry

    lax.fori_loop(0, 4, b_step, 0)

    lane = lax.broadcasted_iota(jnp.int32, (8, 128), 1)

    def put(i, which):
        res, out = ((res_re, out_re), (res_im, out_im))[which]
        rows = pl.ds(pl.multiple_of(256 * i, 256), 256)
        return pltpu.make_async_copy(res.at[rows], out.at[rows], sem.at[which, i])

    def a_step(i, carry):
        rows = pl.ds(pl.multiple_of(8 * i, 8), 8)
        res = fft([(zb[a, rows, 0:128], zb[a, rows, 128:256]) for a in range(32)])
        for j in range(8):
            for part, out in ((0, res_re), (1, res_im)):
                moved = swap_groups([res[4 * j + t][part] for t in range(4)], lane)
                for kc in range(4):
                    out[pl.ds(i * 256 + j * 4 + kc, 8, stride=32), :] = moved[kc]
        put(i, 0).start()
        put(i, 1).start()
        return carry

    lax.fori_loop(0, 4, a_step, 0)
    for i in range(4):
        put(i, 0).wait()
        put(i, 1).wait()


def on_device(occ, vir, docc, dvir):
    anyspace = pl.BlockSpec(memory_space=pl.ANY)
    vmem = pl.BlockSpec(memory_space=pltpu.VMEM)
    dma = pltpu.SemaphoreType.DMA
    xr, ntab = pl.pallas_call(
        kernel,
        out_shape=(pltpu.VMEM((64, 32, 128), BF16), pltpu.VMEM((256, 256), BF16)),
        in_specs=[anyspace] * 6,
        out_specs=(vmem, vmem),
        scratch_shapes=[
            pltpu.VMEM((48, 4096), BF16),
            pltpu.VMEM((1, 1024), F32),
            pltpu.VMEM((1, 512), F32),
            pltpu.VMEM((32, 1024), F32),
            pltpu.VMEM((512, 1024), BF16),
            pltpu.VMEM((8, 48, 512), BF16),
            pltpu.VMEM((4, 8, 48, 512), BF16),
            pltpu.VMEM((48, 1024), BF16),
            pltpu.VMEM((2, 4, 8, 48, 128), BF16),
            pltpu.VMEM((256, 1024), BF16),
            dma((6,)),
            dma, dma((8,)),
            dma, dma((8,)),
            dma, dma,
            dma, dma,
            dma, dma((8,)),
            dma, dma((8,)),
            dma, dma((2,)),
            dma, dma,
            pltpu.SemaphoreType.REGULAR,
        ],
        compiler_params=pltpu.CompilerParams(collective_id=0, has_side_effects=True),
    )(
        occ, vir, docc.reshape(1, 1024), dvir.reshape(1, 512),
        jnp.asarray(c_table()), jnp.asarray(b_table()).astype(BF16),
    )
    out = jax.ShapeDtypeStruct((1024, 128), F32)
    res = pl.pallas_call(
        finish,
        out_shape=(out, out),
        in_specs=[vmem, vmem],
        out_specs=(anyspace, anyspace),
        scratch_shapes=[
            pltpu.VMEM((32, 32, 256), F32),
            pltpu.VMEM((1024, 128), F32),
            pltpu.VMEM((1024, 128), F32),
            dma((2, 4)),
        ],
    )(pltpu.with_memory_space_constraint(xr, pltpu.VMEM), pltpu.with_memory_space_constraint(ntab, pltpu.VMEM))

    def placed(part):
        return jnp.transpose(part.reshape(32, 8, 4, 128), (0, 2, 1, 3)).reshape(32, 4, 1024)

    return placed(res[0]), placed(res[1])


def solution(mesh):
    in_specs = (P("row", "col"), P("row", "col"), P(), P())
    out_specs = (P("row", "col", None), P("row", "col", None))
    return jax.shard_map(
        on_device, mesh=mesh, in_specs=in_specs, out_specs=out_specs, check_vma=False
    )
```

time: 54 us -> 48.9 us (0.906)
  Pallas kernels: 53.2 us -> 48.1 us
    pallas_call x1, Pallas kernels: 49.1 us -> 45.3 us  [on_device(): pl.pallas_call(kernel, out_shape=(pltpu.VMEM((64, 32, 128), BF16), pltpu....]
    pallas_call x1, Pallas kernels: 4.05 us -> 2.9 us  [on_device(): pl.pallas_call(finish, out_shape=(out, out), in_specs=[vmem, vmem], out_s...]
where the time goes in v5:
time: 48.9 us; the launch traced here: 48.8 us
  Pallas kernels  48.1 us (98%)
  between operations  0.64 us (1%)
    pallas_call x1, Pallas kernels, on_device(): pl.pallas_call(kernel, out_shape=(pltpu.VMEM((64, 32, 128), BF16), pltpu....  45.3 us
    pallas_call x1, Pallas kernels, on_device(): pl.pallas_call(finish, out_shape=(out, out), in_specs=[vmem, vmem], out_s...  2.9 us

profile of v5, /device:TPU:1, one launch (start us, length us, event | category | flops | bytes accessed | tf_op | source)
XLA Modules:
  0.0 48.8 jit_solution(4826315434107209653)
XLA Ops:
  0.6 45.3 %shard_map.77 = (bf16[64,32,128]{2,1,0:T(8,128)(2,1)S(1)}, bf16[256,256]{1,0:T(8,128)(2,1)S(1)}) custom-call(bf16[32,4096]{1,0:T(8,128)(2,1)} %occ.1, bf16[16,4096]{1,0:T(8,128)(2,1)} %vir.1, f32[1,1024]{1,0:T(1,128)} %bitcast.12, f32[1,512]{1,0:T(1,128)} %bitcast.13, f32[32,1024]{1,0:T(8,128)} %constant.4.clone.ctab, bf16[256,256]{1,0:T(8,128)(2,1)} %constant.7.btab), custom_call_target="tpu_custom_call" | custom-call | tf_op jit(solution)/shard_map/pallas_call | solution.py:409
  45.9 2.9 %shard_map.78 = (f32[1024,128]{1,0:T(8,128)}, f32[1024,128]{1,0:T(8,128)}) custom-call(bf16[64,32,128]{2,1,0:T(8,128)(2,1)S(1)} %get-tuple-element.6.xr, bf16[256,256]{1,0:T(8,128)(2,1)S(1)} %get-tuple-element.7.ntab), custom_call_target="tpu_custom_call" | custom-call | tf_op jit(solution)/shard_map/pallas_call | solution.py:442

commit v6 on v5

--- a/solution.py
+++ b/solution.py
@@ -33,15 +33,15 @@
 
 def b_table():
     cos, sin = angle_table(32)
-    table = np.zeros((2, 2, 16, 4, 2, 4, 32), np.float32)
+    c, s = cos.reshape(4, 8, 32), sin.reshape(4, 8, 32)
+    table = np.zeros((4, 2, 2, 8, 4, 2, 2, 4, 32), np.float32)
     for kc in range(4):
-        c = cos.reshape(2, 16, 32)
-        s = sin.reshape(2, 16, 32)
-        table[:, 0, :, kc, 0, kc, :] = c
-        table[:, 0, :, kc, 1, kc, :] = -s
-        table[:, 1, :, kc, 0, kc, :] = s
-        table[:, 1, :, kc, 1, kc, :] = c
-    return table.reshape(256, 256)
+        for h in range(2):
+            table[:, 0, h, :, kc, h, 0, kc, :] = c
+            table[:, 0, h, :, kc, h, 1, kc, :] = -s
+            table[:, 1, h, :, kc, h, 0, kc, :] = s
+            table[:, 1, h, :, kc, h, 1, kc, :] = c
+    return table.reshape(512, 512)
 
 
 def fft(parts):
@@ -193,25 +193,28 @@
         for dy in (1, 3, 2):
             c_copy(o, zs, dy).start()
 
-    def p1_copy(dz):
+    def part(zs, p):
+        return pl.ds(pl.multiple_of(zs * 512 + p * 256, 256), 256)
+
+    def p1_copy(p, dz):
         zt = lax.rem(z + dz, 8)
-        lanes = pl.ds(pl.multiple_of(zt * 512, 512), 512)
-        return pltpu.make_async_remote_copy(
-            src_ref=inb.at[:, lanes], dst_ref=pz.at[z], send_sem=p1s, recv_sem=p1r.at[z],
+        return pltpu.make_async_remote_copy(
+            src_ref=inb.at[:, part(zt, p)], dst_ref=pz.at[p, z], send_sem=p1s, recv_sem=p1r.at[p, z],
             device_id=(row_of(xh, zt, core), col), device_id_type=MESH,
         )
 
-    def p2_copy(src, zs, side):
+    def p2_copy(src, p, zs, side):
         xt = lax.rem(x + 1 + 2 * side, 4)
         return pltpu.make_async_remote_copy(
-            src_ref=src, dst_ref=pb.at[2 * xh + core, zs], send_sem=p2s, recv_sem=p2r.at[zs],
+            src_ref=src, dst_ref=pb.at[p, 2 * xh + core, zs], send_sem=p2s, recv_sem=p2r.at[p, zs],
             device_id=(row_of(lax.div(xt, 2), z, core), lax.rem(xt, 2) * 4 + y), device_id_type=MESH,
         )
 
-    def p3_copy(xs, zs):
-        return pltpu.make_async_remote_copy(
-            src_ref=pb.at[2 * xs + core, zs], dst_ref=pb.at[2 * xs + core, zs], send_sem=p3s,
-            recv_sem=p3r, device_id=(row + 1 - 2 * core, col), device_id_type=MESH,
+    def p3_copy(p, xs, zs):
+        ref = pb.at[p, 2 * xs + core, zs]
+        return pltpu.make_async_remote_copy(
+            src_ref=ref, dst_ref=ref, send_sem=p3s, recv_sem=p3r.at[p],
+            device_id=(row + 1 - 2 * core, col), device_id_type=MESH,
         )
 
     self_a = jnp.logical_and(col == 0, jnp.logical_and(xh == 0, core == 0))
@@ -231,12 +234,11 @@
     def _():
         rc[0, 0, z] = rs[:, 0:128]
 
-    for dz in NEAR:
-        p1_copy(dz).start()
-
-    mine = pl.ds(pl.multiple_of(z * 512, 512), 512)
-    for side in range(2):
-        p2_copy(inb.at[:, mine], z, side).start()
+    for dz in DIST:
+        p1_copy(0, dz).start()
+    for p in range(2):
+        for side in range(2):
+            p2_copy(inb.at[:, part(z, p)], p, z, side).start()
 
     @pl.when(jnp.logical_not(self_a))
     def _():
@@ -246,8 +248,8 @@
         b_copy(dz).start()
     near_y(0, z)
     x_copy(z).start()
-    for dz in FAR:
-        p1_copy(dz).start()
+    for dz in DIST:
+        p1_copy(1, dz).start()
 
     blane = lax.rem(lax.div(lax.broadcasted_iota(jnp.int32, (32, 1024), 1), 4), 16)
     ct = ctv[...]
@@ -262,80 +264,90 @@
     def source(dz):
         return lax.rem(z + 8 - dz, 8)
 
-    def relay(dz):
+    def relay(p, dz):
         zs = source(dz)
-        landed(pz.at[zs], p1r.at[zs])
-        p2_copy(pz.at[zs], zs, 0).start()
-        p2_copy(pz.at[zs], zs, 1).start()
-
-    def forward(dz):
+        landed(pz.at[p, zs], p1r.at[p, zs])
+        p2_copy(pz.at[p, zs], p, zs, 0).start()
+        p2_copy(pz.at[p, zs], p, zs, 1).start()
+
+    def forward(p, dz):
         zs = source(dz)
-        landed(pb.at[pl.ds(0, 2), zs], p2r.at[zs])
-        p3_copy(0, zs).start()
-        p3_copy(1, zs).start()
+        landed(pb.at[p, pl.ds(0, 2), zs], p2r.at[p, zs])
+        p3_copy(p, 0, zs).start()
+        p3_copy(p, 1, zs).start()
+
+    slot = ((1 - xl) * 4 + y) * 8 + z
+    has_self = lax.div(z, 4) == core
+
+    def y_copy(p, o, i, c):
+        rows = pl.ds(pl.multiple_of(i * 16, 16), 16)
+        lanes = pl.ds(pl.multiple_of(c * 128, 128), 128)
+        return pltpu.make_async_remote_copy(
+            src_ref=yb.at[p, o, rows, lanes], dst_ref=xr.at[slot, p], send_sem=ys, recv_sem=yr,
+            device_id=(16 * xh + 8 * core + 4 * half(o) + i, c), device_id_type=MESH,
+        )
+
+    def half(o):
+        return xl + o - 2 * xl * o
+
+    def multiply(p, o):
+        acc_o = jnp.zeros((128, 256), F32)
+        acc_v = jnp.zeros((128, 256), F32)
+        for b in range(4):
+            acc_o += tdot(rc[o, b, :, 0:32, :].reshape(256, 128), pb[p, b, :, 0:32, :].reshape(256, 256))
+            acc_v += tdot(rc[o, b, :, 32:48, :].reshape(128, 128), pb[p, b, :, 32:48, :].reshape(128, 256))
+        polar = (acc_o * acc_v * SCALE).astype(BF16).reshape(4, 2, 16, 256)
+        both = jnp.concatenate([polar[:, 0].reshape(64, 256), polar[:, 1].reshape(64, 256)], axis=1)
+        yb[p, o] = mdot(both, mtab[...]).astype(BF16)
+
+        def y_send(j, carry):
+            i = lax.rem(j, 4)
+            c = lax.rem(lax.div(j, 4) + col, 8)
+
+            @pl.when(jnp.logical_or(16 * xh + 8 * core + 4 * half(o) + i != row, c != col))
+            def _():
+                y_copy(p, o, i, c).start()
+
+            return carry
+
+        lax.fori_loop(0, 32, y_send, 0)
 
     for dz in NEAR:
-        relay(dz)
+        relay(0, dz)
     for dz in DIST:
         zs = source(dz)
         landed(rc.at[0, y, zs], rbr.at[zs])
         near_y(0, zs)
         x_copy(zs).start()
     for dz in FAR:
-        relay(dz)
-    for dz in (0, *NEAR):
-        forward(dz)
+        relay(0, dz)
     for dz in (0, *DIST):
         zs = source(dz)
         landed(rc.at[1, y, zs], rxr.at[zs])
         near_y(1, zs)
-    for dz in FAR:
-        forward(dz)
-    landed(pb.at[pl.ds(0, 2)], p3r)
-
-    slot = ((1 - xl) * 4 + y) * 8 + z
-    has_self = lax.div(z, 4) == core
-
-    def y_copy(o, i, c):
-        rows = pl.ds(pl.multiple_of(o * 128 + i * 32, 32), 32)
-        lanes = pl.ds(pl.multiple_of(c * 128, 128), 128)
-        return pltpu.make_async_remote_copy(
-            src_ref=yb.at[rows, lanes], dst_ref=xr.at[slot], send_sem=ys, recv_sem=yr,
-            device_id=(16 * xh + 8 * core + 4 * half(o) + i, c), device_id_type=MESH,
-        )
-
-    def half(o):
-        return xl + o - 2 * xl * o
-
+    for dz in (0, *DIST):
+        forward(0, dz)
+    for dz in DIST:
+        relay(1, dz)
+    landed(pb.at[0, pl.ds(0, 2)], p3r.at[0])
+    landed(rc.at[0, pl.ds(0, 3)], rcr.at[0])
     pl.semaphore_wait(ready, 16)
-    for o in range(2):
-        landed(rc.at[o, pl.ds(0, 3)], rcr.at[o])
-        acc_o = jnp.zeros((128, 512), F32)
-        acc_v = jnp.zeros((128, 512), F32)
-        for b in range(4):
-            acc_o += tdot(rc[o, b, :, 0:32, :].reshape(256, 128), pb[b, :, 0:32, :].reshape(256, 512))
-            acc_v += tdot(rc[o, b, :, 32:48, :].reshape(128, 128), pb[b, :, 32:48, :].reshape(128, 512))
-        polar = (acc_o * acc_v * SCALE).astype(BF16)
-        yb[128 * o : 128 * o + 128, :] = mdot(polar, mtab[...]).astype(BF16)
-
-        def y_send(j, carry):
-            i = lax.rem(j, 4)
-            c = lax.rem(lax.div(j, 4) + col, 8)
-
-            @pl.when(jnp.logical_or(16 * xh + 8 * core + 4 * half(o) + i != row, c != col))
-            def _():
-                y_copy(o, i, c).start()
-
-            return carry
-
-        lax.fori_loop(0, 32, y_send, 0)
+    multiply(0, 0)
+    for dz in (0, *DIST):
+        forward(1, dz)
+    landed(rc.at[1, pl.ds(0, 3)], rcr.at[1])
+    multiply(0, 1)
+    landed(pb.at[1, pl.ds(0, 2)], p3r.at[1])
+    multiply(1, 0)
+    multiply(1, 1)
 
     @pl.when(has_self)
     def _():
         m = row - 16 * xh - 8 * core
         o = jnp.abs(lax.div(m, 4) - xl)
-        rows = pl.ds(pl.multiple_of(o * 128 + lax.rem(m, 4) * 32, 32), 32)
-        xr[slot] = yb[rows, pl.ds(pl.multiple_of(col * 128, 128), 128)]
+        rows = pl.ds(pl.multiple_of(lax.rem(m, 4) * 16, 16), 16)
+        for p in range(2):
+            xr[slot, p] = yb[p, o, rows, pl.ds(pl.multiple_of(col * 128, 128), 128)]
         landed(xr.at[pl.ds(0, 63)], yr)
 
     @pl.when(jnp.logical_not(has_self))
@@ -350,11 +362,12 @@
     def _():
         landed(rc.at[0, 0, pl.ds(0, 7)], ras)
 
-    landed(pz.at[pl.ds(0, 7)], p1s)
+    for p in range(2):
+        landed(pz.at[p, pl.ds(0, 7)], p1s)
+        landed(pb.at[p, pl.ds(0, 2)], p2s)
+        landed(pb.at[p, pl.ds(0, 2)], p3s)
     landed(rc.at[0, 0, pl.ds(0, 7)], rbs)
     landed(rc.at[0, 0], rxs)
-    landed(pb.at[pl.ds(0, 2)], p2s)
-    landed(pb.at[pl.ds(0, 2)], p3s)
     landed(rc.at[0, pl.ds(0, 3)], rcs)
     landed(rc.at[1, pl.ds(0, 3)], rcs)
 
@@ -369,10 +382,9 @@
 
 def finish(xr, ntab, out_re, out_im, zb, res_re, res_im, sem):
     def b_step(i, carry):
-        part = xr[pl.ds(pl.multiple_of(16 * i, 16), 16)].reshape(8, 2, 32, 128)
-        both = jnp.concatenate([part[:, 0].reshape(256, 128), part[:, 1].reshape(256, 128)], axis=1)
-        res = mdot(both, ntab[...])
-        zb[pl.ds(8 * i, 8)] = res.reshape(8, 32, 256)
+        part = xr[pl.ds(pl.multiple_of(16 * i, 16), 16)].reshape(8, 4, 16, 128)
+        both = jnp.concatenate([part[:, q].reshape(128, 128) for q in range(4)], axis=1)
+        zb[pl.ds(8 * i, 8)] = mdot(both, ntab[...]).reshape(8, 16, 512)
         return carry
 
     lax.fori_loop(0, 4, b_step, 0)
@@ -385,8 +397,10 @@
         return pltpu.make_async_copy(res.at[rows], out.at[rows], sem.at[which, i])
 
     def a_step(i, carry):
-        rows = pl.ds(pl.multiple_of(8 * i, 8), 8)
-        res = fft([(zb[a, rows, 0:128], zb[a, rows, 128:256]) for a in range(32)])
+        rows = pl.ds(pl.multiple_of(8 * lax.rem(i, 2), 8), 8)
+        real = pl.ds(pl.multiple_of(256 * lax.div(i, 2), 128), 128)
+        imag = pl.ds(pl.multiple_of(256 * lax.div(i, 2) + 128, 128), 128)
+        res = fft([(zb[a, rows, real], zb[a, rows, imag]) for a in range(32)])
         for j in range(8):
             for part, out in ((0, res_re), (1, res_im)):
                 moved = swap_groups([res[4 * j + t][part] for t in range(4)], lane)
@@ -408,7 +422,7 @@
     dma = pltpu.SemaphoreType.DMA
     xr, ntab = pl.pallas_call(
         kernel,
-        out_shape=(pltpu.VMEM((64, 32, 128), BF16), pltpu.VMEM((256, 256), BF16)),
+        out_shape=(pltpu.VMEM((64, 2, 16, 128), BF16), pltpu.VMEM((512, 512), BF16)),
         in_specs=[anyspace] * 6,
         out_specs=(vmem, vmem),
         scratch_shapes=[
@@ -417,15 +431,15 @@
             pltpu.VMEM((1, 512), F32),
             pltpu.VMEM((32, 1024), F32),
             pltpu.VMEM((512, 1024), BF16),
-            pltpu.VMEM((8, 48, 512), BF16),
-            pltpu.VMEM((4, 8, 48, 512), BF16),
+            pltpu.VMEM((2, 8, 48, 256), BF16),
+            pltpu.VMEM((2, 4, 8, 48, 256), BF16),
             pltpu.VMEM((48, 1024), BF16),
             pltpu.VMEM((2, 4, 8, 48, 128), BF16),
-            pltpu.VMEM((256, 1024), BF16),
+            pltpu.VMEM((2, 2, 64, 1024), BF16),
             dma((6,)),
-            dma, dma((8,)),
-            dma, dma((8,)),
-            dma, dma,
+            dma, dma((2, 8)),
+            dma, dma((2, 8)),
+            dma, dma((2,)),
             dma, dma,
             dma, dma((8,)),
             dma, dma((8,)),
@@ -445,7 +459,7 @@
         in_specs=[vmem, vmem],
         out_specs=(anyspace, anyspace),
         scratch_shapes=[
-            pltpu.VMEM((32, 32, 256), F32),
+            pltpu.VMEM((32, 16, 512), F32),
             pltpu.VMEM((1024, 128), F32),
             pltpu.VMEM((1024, 128), F32),
             dma((2, 4)),

time: 48.9 us -> 48.1 us (0.984)
  Pallas kernels: 48.1 us -> 47.3 us
    pallas_call x1, Pallas kernels: 45.3 us -> 44.2 us  [on_device(): pl.pallas_call(kernel, out_shape=(pltpu.VMEM((64, 2, 16, 128), BF16), plt...]
where the time goes in v6:
time: 48.1 us; the launch traced here: 48 us
  Pallas kernels  47.3 us (98%)
  between operations  0.64 us (1%)
    pallas_call x1, Pallas kernels, on_device(): pl.pallas_call(kernel, out_shape=(pltpu.VMEM((64, 2, 16, 128), BF16), plt...  44.2 us
    pallas_call x1, Pallas kernels, on_device(): pl.pallas_call(finish, out_shape=(out, out), in_specs=[vmem, vmem], out_s...  3.1 us

profile of v6, /device:TPU:1, one launch (start us, length us, event | category | flops | bytes accessed | tf_op | source)
XLA Modules:
  0.0 48.0 jit_solution(2376948189457995724)
XLA Ops:
  0.6 44.2 %shard_map.77 = (bf16[64,2,16,128]{3,2,1,0:T(8,128)(2,1)S(1)}, bf16[512,512]{1,0:T(8,128)(2,1)S(1)}) custom-call(bf16[32,4096]{1,0:T(8,128)(2,1)} %occ.1, bf16[16,4096]{1,0:T(8,128)(2,1)} %vir.1, f32[1,1024]{1,0:T(1,128)} %bitcast.12, f32[1,512]{1,0:T(1,128)} %bitcast.13, f32[32,1024]{1,0:T(8,128)} %constant.4.clone.ctab, bf16[512,512]{1,0:T(8,128)(2,1)} %constant.7.btab), custom_call_target="tpu_custom_call" | custom-call | tf_op jit(solution)/shard_map/pallas_call | solution.py:423
  44.9 3.1 %shard_map.78 = (f32[1024,128]{1,0:T(8,128)}, f32[1024,128]{1,0:T(8,128)}) custom-call(bf16[64,2,16,128]{3,2,1,0:T(8,128)(2,1)S(1)} %get-tuple-element.6.xr, bf16[512,512]{1,0:T(8,128)(2,1)S(1)} %get-tuple-element.7.ntab), custom_call_target="tpu_custom_call" | custom-call | tf_op jit(solution)/shard_map/pallas_call | solution.py:456

commit v7 on v5

--- a/solution.py
+++ b/solution.py
@@ -85,10 +85,10 @@
 
 
 def kernel(
-    occ, vir, docc, dvir, ctab, btab, xr, ntab,
-    inb, dov, dvv, ctv, mtab,
-    pz, pb, rs, rc, yb,
-    in_sem, p1s, p1r, p2s, p2r, p3s, p3r, ras, rar, rbs, rbr, rxs, rxr, rcs, rcr, ys, yr, ready,
+    occ, vir, docc, dvir, ctab, btab, zb,
+    inb, dov, dvv, ctv, mtab, ntab,
+    pz, pb, rs, rc, rto, rtv, gp, pr, xs, xr,
+    in_sem, p1s, p1r, p2s, p2r, p3s, p3r, ras, rar, rbs, rbr, rxs, rxr, rcs, rcr, gs, gr, ys, yr, ready,
 ):
     row, col = lax.axis_index("row"), lax.axis_index("col")
     core = lax.rem(row, 2)
@@ -193,25 +193,30 @@
         for dy in (1, 3, 2):
             c_copy(o, zs, dy).start()
 
-    def p1_copy(dz):
+    def lanes_of(p):
+        return pl.ds(0, 512) if p is None else pl.ds(256 * p, 256)
+
+    def p1_copy(dz, p=None):
         zt = lax.rem(z + dz, 8)
-        lanes = pl.ds(pl.multiple_of(zt * 512, 512), 512)
-        return pltpu.make_async_remote_copy(
-            src_ref=inb.at[:, lanes], dst_ref=pz.at[z], send_sem=p1s, recv_sem=p1r.at[z],
-            device_id=(row_of(xh, zt, core), col), device_id_type=MESH,
-        )
-
-    def p2_copy(src, zs, side):
+        start, size = (0, 512) if p is None else (256 * p, 256)
+        lanes = pl.ds(pl.multiple_of(zt * 512 + start, 256), size)
+        return pltpu.make_async_remote_copy(
+            src_ref=inb.at[:, lanes], dst_ref=pz.at[z, :, lanes_of(p)], send_sem=p1s,
+            recv_sem=p1r.at[z, p or 0], device_id=(row_of(xh, zt, core), col), device_id_type=MESH,
+        )
+
+    def p2_copy(src, zs, side, p=None):
         xt = lax.rem(x + 1 + 2 * side, 4)
         return pltpu.make_async_remote_copy(
-            src_ref=src, dst_ref=pb.at[2 * xh + core, zs], send_sem=p2s, recv_sem=p2r.at[zs],
+            src_ref=src, dst_ref=pb.at[2 * xh + core, zs, :, lanes_of(p)], send_sem=p2s, recv_sem=p2r.at[zs, p or 0],
             device_id=(row_of(lax.div(xt, 2), z, core), lax.rem(xt, 2) * 4 + y), device_id_type=MESH,
         )
 
-    def p3_copy(xs, zs):
-        return pltpu.make_async_remote_copy(
-            src_ref=pb.at[2 * xs + core, zs], dst_ref=pb.at[2 * xs + core, zs], send_sem=p3s,
-            recv_sem=p3r, device_id=(row + 1 - 2 * core, col), device_id_type=MESH,
+    def p3_copy(xs, zs, p=None):
+        ref = pb.at[2 * xs + core, zs, :, lanes_of(p)]
+        return pltpu.make_async_remote_copy(
+            src_ref=ref, dst_ref=ref, send_sem=p3s, recv_sem=p3r,
+            device_id=(row + 1 - 2 * core, col), device_id_type=MESH,
         )
 
     self_a = jnp.logical_and(col == 0, jnp.logical_and(xh == 0, core == 0))
@@ -246,8 +251,9 @@
         b_copy(dz).start()
     near_y(0, z)
     x_copy(z).start()
-    for dz in FAR:
-        p1_copy(dz).start()
+    for p in range(2):
+        for dz in FAR:
+            p1_copy(dz, p).start()
 
     blane = lax.rem(lax.div(lax.broadcasted_iota(jnp.int32, (32, 1024), 1), 4), 16)
     ct = ctv[...]
@@ -262,85 +268,137 @@
     def source(dz):
         return lax.rem(z + 8 - dz, 8)
 
-    def relay(dz):
+    def relay(dz, p=None):
         zs = source(dz)
-        landed(pz.at[zs], p1r.at[zs])
-        p2_copy(pz.at[zs], zs, 0).start()
-        p2_copy(pz.at[zs], zs, 1).start()
-
-    def forward(dz):
+        ref = pz.at[zs, :, lanes_of(p)]
+        landed(ref, p1r.at[zs, p or 0])
+        p2_copy(ref, zs, 0, p).start()
+        p2_copy(ref, zs, 1, p).start()
+
+    def forward(dz, p=None):
         zs = source(dz)
-        landed(pb.at[pl.ds(0, 2), zs], p2r.at[zs])
-        p3_copy(0, zs).start()
-        p3_copy(1, zs).start()
-
-    for dz in NEAR:
-        relay(dz)
-    for dz in DIST:
+        landed(pb.at[pl.ds(0, 2), zs, :, lanes_of(p)], p2r.at[zs, p or 0])
+        p3_copy(0, zs, p).start()
+        p3_copy(1, zs, p).start()
+
+    def gathered_z(dz):
         zs = source(dz)
         landed(rc.at[0, y, zs], rbr.at[zs])
         near_y(0, zs)
         x_copy(zs).start()
-    for dz in FAR:
-        relay(dz)
-    for dz in (0, *NEAR):
-        forward(dz)
-    for dz in (0, *DIST):
+
+    def gathered_x(dz):
         zs = source(dz)
         landed(rc.at[1, y, zs], rxr.at[zs])
         near_y(1, zs)
-    for dz in FAR:
-        forward(dz)
-    landed(pb.at[pl.ds(0, 2)], p3r)
-
-    slot = ((1 - xl) * 4 + y) * 8 + z
-    has_self = lax.div(z, 4) == core
-
-    def y_copy(o, i, c):
-        rows = pl.ds(pl.multiple_of(o * 128 + i * 32, 32), 32)
-        lanes = pl.ds(pl.multiple_of(c * 128, 128), 128)
-        return pltpu.make_async_remote_copy(
-            src_ref=yb.at[rows, lanes], dst_ref=xr.at[slot], send_sem=ys, recv_sem=yr,
-            device_id=(16 * xh + 8 * core + 4 * half(o) + i, c), device_id_type=MESH,
-        )
-
-    def half(o):
-        return xl + o - 2 * xl * o
-
-    pl.semaphore_wait(ready, 16)
-    for o in range(2):
+
+    def gathered_y(o):
         landed(rc.at[o, pl.ds(0, 3)], rcr.at[o])
+        for b in range(4):
+            rto[o, :, 256 * b : 256 * b + 256] = rc[o, b, :, 0:32, :].reshape(256, 128).T
+            rtv[o, :, 128 * b : 128 * b + 128] = rc[o, b, :, 32:48, :].reshape(128, 128).T
+
+    def g_copy(t, kk):
+        o = jnp.abs(lax.div(t, 2) - xl)
+        rows = pl.ds(pl.multiple_of(64 * lax.rem(t, 2) + 32 * kk, 32), 32)
+        return pltpu.make_async_remote_copy(
+            src_ref=gp.at[o, rows], dst_ref=pr.at[z], send_sem=gs, recv_sem=gr.at[z],
+            device_id=(row_of(xh, 4 * core + t, kk), col), device_id_type=MESH,
+        )
+
+    def multiply(o):
         acc_o = jnp.zeros((128, 512), F32)
         acc_v = jnp.zeros((128, 512), F32)
         for b in range(4):
-            acc_o += tdot(rc[o, b, :, 0:32, :].reshape(256, 128), pb[b, :, 0:32, :].reshape(256, 512))
-            acc_v += tdot(rc[o, b, :, 32:48, :].reshape(128, 128), pb[b, :, 32:48, :].reshape(128, 512))
-        polar = (acc_o * acc_v * SCALE).astype(BF16)
-        yb[128 * o : 128 * o + 128, :] = mdot(polar, mtab[...]).astype(BF16)
+            acc_o += mdot(rto[o, :, 256 * b : 256 * b + 256], pb[b, :, 0:32, :].reshape(256, 512))
+            acc_v += mdot(rtv[o, :, 128 * b : 128 * b + 128], pb[b, :, 32:48, :].reshape(128, 512))
+        gp[o] = (acc_o * acc_v * SCALE).astype(BF16)
+
+    for dz in NEAR:
+        relay(dz)
+    for dz in DIST:
+        gathered_z(dz)
+    for dz in FAR:
+        relay(dz, 0)
+    for dz in (0, *DIST):
+        gathered_x(dz)
+    for dz in FAR:
+        relay(dz, 1)
+    for dz in (0, *NEAR):
+        forward(dz)
+    for p in range(2):
+        for dz in FAR:
+            forward(dz, p)
+    gathered_y(0)
+    gathered_y(1)
+    pl.semaphore_wait(ready, 16)
+    landed(pb.at[pl.ds(0, 2)], p3r)
+    multiply(0)
+    multiply(1)
+
+    own = lax.div(z, 4) == core
+    place = lax.rem(z, 4)
+    for j in range(4):
+        inner = jnp.logical_or(place == 1, place == 2)
+
+        def nearest(j):
+            t = jnp.where(inner, 1 - j if j < 2 else j, j)
+            return jnp.where(place >= 2, 3 - t, t)
+
+        t = jnp.where(own, nearest(j), nearest(3 - j))
+        for kk in range(2):
+            mine = row == row_of(xh, 4 * core + t, kk)
+
+            @pl.when(jnp.logical_not(mine))
+            def _():
+                g_copy(t, kk).start()
+
+            @pl.when(mine)
+            def _():
+                o = jnp.abs(lax.div(t, 2) - xl)
+                pr[z] = gp[o, pl.ds(pl.multiple_of(64 * lax.rem(t, 2) + 32 * kk, 32), 32)]
+
+    slot = 8 * ((1 - xl) * 4 + y)
+
+    def y_copy(q, c):
+        lanes = pl.ds(pl.multiple_of(c * 128, 128), 128)
+        return pltpu.make_async_remote_copy(
+            src_ref=xs.at[pl.ds(2 * q, 2), :, lanes], dst_ref=xr.at[pl.ds(slot + 2 * q, 2)],
+            send_sem=ys, recv_sem=yr.at[q], device_id=(row, c), device_id_type=MESH,
+        )
+
+    def pair(g):
+        near = 3 - 2 * lax.rem(z, 2)
+        return lax.rem(lax.div(z, 2) + (0, near, 4 - near, 2)[g], 4)
+
+    for g in range(4):
+        q = pair(g)
+        for t in range(2):
+            zs = 2 * q + t
+
+            @pl.when(jnp.logical_or(zs != z, jnp.logical_not(own)))
+            def _():
+                landed(pr.at[zs], gr.at[zs])
+
+        part = pr[pl.ds(2 * q, 2)].reshape(64, 512)
+        xs[pl.ds(2 * q, 2)] = mdot(part, mtab[...]).astype(BF16).reshape(2, 32, 1024)
 
         def y_send(j, carry):
-            i = lax.rem(j, 4)
-            c = lax.rem(lax.div(j, 4) + col, 8)
-
-            @pl.when(jnp.logical_or(16 * xh + 8 * core + 4 * half(o) + i != row, c != col))
-            def _():
-                y_copy(o, i, c).start()
-
+            y_copy(q, lax.rem(col + j, 8)).start()
             return carry
 
-        lax.fori_loop(0, 32, y_send, 0)
-
-    @pl.when(has_self)
-    def _():
-        m = row - 16 * xh - 8 * core
-        o = jnp.abs(lax.div(m, 4) - xl)
-        rows = pl.ds(pl.multiple_of(o * 128 + lax.rem(m, 4) * 32, 32), 32)
-        xr[slot] = yb[rows, pl.ds(pl.multiple_of(col * 128, 128), 128)]
-        landed(xr.at[pl.ds(0, 63)], yr)
-
-    @pl.when(jnp.logical_not(has_self))
-    def _():
-        landed(xr, yr)
+        lax.fori_loop(1, 8, y_send, 0)
+        lanes = pl.ds(pl.multiple_of(col * 128, 128), 128)
+        xr[pl.ds(slot + 2 * q, 2)] = xs[pl.ds(2 * q, 2), :, lanes]
+
+    for g in range(4):
+        q = pair(g)
+        landed(xr.at[pl.ds(0, 14)], yr.at[q])
+        parts = [xr[8 * c + 2 * q + t] for t in range(2) for c in range(8)]
+        both = jnp.concatenate([jnp.concatenate(parts[8 * t : 8 * t + 8], axis=0) for t in range(2)], axis=1)
+        res = mdot(both, ntab[...])
+        for c in range(8):
+            zb[4 * c + q] = res[32 * c : 32 * c + 32]
 
     @pl.when(jnp.logical_and(col == 0, jnp.logical_not(self_a)))
     def _():
@@ -358,25 +416,18 @@
     landed(rc.at[0, pl.ds(0, 3)], rcs)
     landed(rc.at[1, pl.ds(0, 3)], rcs)
 
-    @pl.when(has_self)
-    def _():
-        landed(xr.at[pl.ds(0, 63)], ys)
-
-    @pl.when(jnp.logical_not(has_self))
-    def _():
-        landed(xr, ys)
-
-
-def finish(xr, ntab, out_re, out_im, zb, res_re, res_im, sem):
-    def b_step(i, carry):
-        part = xr[pl.ds(pl.multiple_of(16 * i, 16), 16)].reshape(8, 2, 32, 128)
-        both = jnp.concatenate([part[:, 0].reshape(256, 128), part[:, 1].reshape(256, 128)], axis=1)
-        res = mdot(both, ntab[...])
-        zb[pl.ds(8 * i, 8)] = res.reshape(8, 32, 256)
-        return carry
-
-    lax.fori_loop(0, 4, b_step, 0)
-
+    landed(xr.at[pl.ds(0, 56)], ys)
+
+    @pl.when(own)
+    def _():
+        landed(pr.at[pl.ds(0, 7)], gs)
+
+    @pl.when(jnp.logical_not(own))
+    def _():
+        landed(pr, gs)
+
+
+def finish(zb, out_re, out_im, res_re, res_im, sem):
     lane = lax.broadcasted_iota(jnp.int32, (8, 128), 1)
 
     def put(i, which):
@@ -406,31 +457,38 @@
     anyspace = pl.BlockSpec(memory_space=pl.ANY)
     vmem = pl.BlockSpec(memory_space=pltpu.VMEM)
     dma = pltpu.SemaphoreType.DMA
-    xr, ntab = pl.pallas_call(
+    zb = pl.pallas_call(
         kernel,
-        out_shape=(pltpu.VMEM((64, 32, 128), BF16), pltpu.VMEM((256, 256), BF16)),
+        out_shape=pltpu.VMEM((32, 32, 256), F32),
         in_specs=[anyspace] * 6,
-        out_specs=(vmem, vmem),
+        out_specs=vmem,
         scratch_shapes=[
             pltpu.VMEM((48, 4096), BF16),
             pltpu.VMEM((1, 1024), F32),
             pltpu.VMEM((1, 512), F32),
             pltpu.VMEM((32, 1024), F32),
             pltpu.VMEM((512, 1024), BF16),
+            pltpu.VMEM((256, 256), BF16),
             pltpu.VMEM((8, 48, 512), BF16),
             pltpu.VMEM((4, 8, 48, 512), BF16),
             pltpu.VMEM((48, 1024), BF16),
             pltpu.VMEM((2, 4, 8, 48, 128), BF16),
-            pltpu.VMEM((256, 1024), BF16),
+            pltpu.VMEM((2, 128, 1024), BF16),
+            pltpu.VMEM((2, 128, 512), BF16),
+            pltpu.VMEM((2, 128, 512), BF16),
+            pltpu.VMEM((8, 32, 512), BF16),
+            pltpu.VMEM((8, 32, 1024), BF16),
+            pltpu.VMEM((64, 32, 128), BF16),
             dma((6,)),
-            dma, dma((8,)),
-            dma, dma((8,)),
+            dma, dma((8, 2)),
+            dma, dma((8, 2)),
             dma, dma,
             dma, dma,
             dma, dma((8,)),
             dma, dma((8,)),
             dma, dma((2,)),
-            dma, dma,
+            dma, dma((8,)),
+            dma, dma((4,)),
             pltpu.SemaphoreType.REGULAR,
         ],
         compiler_params=pltpu.CompilerParams(collective_id=0, has_side_effects=True),
@@ -442,15 +500,14 @@
     res = pl.pallas_call(
         finish,
         out_shape=(out, out),
-        in_specs=[vmem, vmem],
+        in_specs=[vmem],
         out_specs=(anyspace, anyspace),
         scratch_shapes=[
-            pltpu.VMEM((32, 32, 256), F32),
             pltpu.VMEM((1024, 128), F32),
             pltpu.VMEM((1024, 128), F32),
             dma((2, 4)),
         ],
-    )(pltpu.with_memory_space_constraint(xr, pltpu.VMEM), pltpu.with_memory_space_constraint(ntab, pltpu.VMEM))
+    )(pltpu.with_memory_space_constraint(zb, pltpu.VMEM))
 
     def placed(part):
         return jnp.transpose(part.reshape(32, 8, 4, 128), (0, 2, 1, 3)).reshape(32, 4, 1024)

time: 48.9 us -> 47.8 us (0.978)
  Pallas kernels: 48.1 us -> 47 us
    pallas_call x2, Pallas kernels: 48.1 us -> 47 us  [the longest x1 44.9 us: on_device(): pl.pallas_call(kernel, out_shape=pltpu.VMEM((32, 32, 256), F32), in_specs...]
where the time goes in v7:
time: 47.8 us; the launch traced here: 47.7 us
  Pallas kernels  47 us (98%)
  between operations  0.64 us (1%)
    pallas_call x1, Pallas kernels, on_device(): pl.pallas_call(kernel, out_shape=pltpu.VMEM((32, 32, 256), F32), in_specs...  44.9 us
    pallas_call x1, Pallas kernels, on_device(): pl.pallas_call(finish, out_shape=(out, out), in_specs=[vmem], out_specs=(...  2.15 us

profile of v7, /device:TPU:1, one launch (start us, length us, event | category | flops | bytes accessed | tf_op | source)
XLA Modules:
  0.0 47.7 jit_solution(12067390937876334004)
XLA Ops:
  0.6 44.9 %shard_map.77.zb = f32[32,32,256]{2,1,0:T(8,128)S(1)} custom-call(bf16[32,4096]{1,0:T(8,128)(2,1)} %occ.1, bf16[16,4096]{1,0:T(8,128)(2,1)} %vir.1, f32[1,1024]{1,0:T(1,128)} %bitcast.12, f32[1,512]{1,0:T(1,128)} %bitcast.13, f32[32,1024]{1,0:T(8,128)} %constant.4.clone.ctab, bf16[256,256]{1,0:T(8,128)(2,1)} %constant.7.btab), custom_call_target="tpu_custom_call" | custom-call | tf_op jit(solution)/shard_map/pallas_call | solution.py:460
  45.5 2.2 %shard_map.78 = (f32[1024,128]{1,0:T(8,128)}, f32[1024,128]{1,0:T(8,128)}) custom-call(f32[32,32,256]{2,1,0:T(8,128)S(1)} %shard_map.77.zb), custom_call_target="tpu_custom_call" | custom-call | tf_op jit(solution)/shard_map/pallas_call | solution.py:500

commit v8 on v7

--- a/solution.py
+++ b/solution.py
@@ -193,29 +193,27 @@
         for dy in (1, 3, 2):
             c_copy(o, zs, dy).start()
 
-    def lanes_of(p):
-        return pl.ds(0, 512) if p is None else pl.ds(256 * p, 256)
-
-    def p1_copy(dz, p=None):
+    def p1_copy(p, dz):
         zt = lax.rem(z + dz, 8)
-        start, size = (0, 512) if p is None else (256 * p, 256)
-        lanes = pl.ds(pl.multiple_of(zt * 512 + start, 256), size)
-        return pltpu.make_async_remote_copy(
-            src_ref=inb.at[:, lanes], dst_ref=pz.at[z, :, lanes_of(p)], send_sem=p1s,
-            recv_sem=p1r.at[z, p or 0], device_id=(row_of(xh, zt, core), col), device_id_type=MESH,
-        )
-
-    def p2_copy(src, zs, side, p=None):
+        return pltpu.make_async_remote_copy(
+            src_ref=inb.at[:, part_of(zt, p)], dst_ref=pz.at[p, z], send_sem=p1s, recv_sem=p1r.at[p, z],
+            device_id=(row_of(xh, zt, core), col), device_id_type=MESH,
+        )
+
+    def part_of(zs, p):
+        return pl.ds(pl.multiple_of(zs * 512 + p * 256, 256), 256)
+
+    def p2_copy(src, p, zs, side):
         xt = lax.rem(x + 1 + 2 * side, 4)
         return pltpu.make_async_remote_copy(
-            src_ref=src, dst_ref=pb.at[2 * xh + core, zs, :, lanes_of(p)], send_sem=p2s, recv_sem=p2r.at[zs, p or 0],
+            src_ref=src, dst_ref=pb.at[p, 2 * xh + core, zs], send_sem=p2s, recv_sem=p2r.at[p, zs],
             device_id=(row_of(lax.div(xt, 2), z, core), lax.rem(xt, 2) * 4 + y), device_id_type=MESH,
         )
 
-    def p3_copy(xs, zs, p=None):
-        ref = pb.at[2 * xs + core, zs, :, lanes_of(p)]
-        return pltpu.make_async_remote_copy(
-            src_ref=ref, dst_ref=ref, send_sem=p3s, recv_sem=p3r,
+    def p3_copy(p, xs, zs):
+        ref = pb.at[p, 2 * xs + core, zs]
+        return pltpu.make_async_remote_copy(
+            src_ref=ref, dst_ref=ref, send_sem=p3s, recv_sem=p3r.at[p],
             device_id=(row + 1 - 2 * core, col), device_id_type=MESH,
         )
 
@@ -236,12 +234,11 @@
     def _():
         rc[0, 0, z] = rs[:, 0:128]
 
-    for dz in NEAR:
-        p1_copy(dz).start()
-
-    mine = pl.ds(pl.multiple_of(z * 512, 512), 512)
-    for side in range(2):
-        p2_copy(inb.at[:, mine], z, side).start()
+    for dz in DIST:
+        p1_copy(0, dz).start()
+    for p in range(2):
+        for side in range(2):
+            p2_copy(inb.at[:, part_of(z, p)], p, z, side).start()
 
     @pl.when(jnp.logical_not(self_a))
     def _():
@@ -251,9 +248,8 @@
         b_copy(dz).start()
     near_y(0, z)
     x_copy(z).start()
-    for p in range(2):
-        for dz in FAR:
-            p1_copy(dz, p).start()
+    for dz in DIST:
+        p1_copy(1, dz).start()
 
     blane = lax.rem(lax.div(lax.broadcasted_iota(jnp.int32, (32, 1024), 1), 4), 16)
     ct = ctv[...]
@@ -268,18 +264,17 @@
     def source(dz):
         return lax.rem(z + 8 - dz, 8)
 
-    def relay(dz, p=None):
+    def relay(p, dz):
         zs = source(dz)
-        ref = pz.at[zs, :, lanes_of(p)]
-        landed(ref, p1r.at[zs, p or 0])
-        p2_copy(ref, zs, 0, p).start()
-        p2_copy(ref, zs, 1, p).start()
-
-    def forward(dz, p=None):
+        landed(pz.at[p, zs], p1r.at[p, zs])
+        p2_copy(pz.at[p, zs], p, zs, 0).start()
+        p2_copy(pz.at[p, zs], p, zs, 1).start()
+
+    def forward(p, dz):
         zs = source(dz)
-        landed(pb.at[pl.ds(0, 2), zs, :, lanes_of(p)], p2r.at[zs, p or 0])
-        p3_copy(0, zs, p).start()
-        p3_copy(1, zs, p).start()
+        landed(pb.at[p, pl.ds(0, 2), zs], p2r.at[p, zs])
+        p3_copy(p, 0, zs).start()
+        p3_copy(p, 1, zs).start()
 
     def gathered_z(dz):
         zs = source(dz)
@@ -295,68 +290,74 @@
     def gathered_y(o):
         landed(rc.at[o, pl.ds(0, 3)], rcr.at[o])
         for b in range(4):
-            rto[o, :, 256 * b : 256 * b + 256] = rc[o, b, :, 0:32, :].reshape(256, 128).T
-            rtv[o, :, 128 * b : 128 * b + 128] = rc[o, b, :, 32:48, :].reshape(128, 128).T
-
-    def g_copy(t, kk):
+            rto[128 * o : 128 * o + 128, 256 * b : 256 * b + 256] = rc[o, b, :, 0:32, :].reshape(256, 128).T
+            rtv[128 * o : 128 * o + 128, 128 * b : 128 * b + 128] = rc[o, b, :, 32:48, :].reshape(128, 128).T
+
+    def g_rows(t, kk):
         o = jnp.abs(lax.div(t, 2) - xl)
-        rows = pl.ds(pl.multiple_of(64 * lax.rem(t, 2) + 32 * kk, 32), 32)
-        return pltpu.make_async_remote_copy(
-            src_ref=gp.at[o, rows], dst_ref=pr.at[z], send_sem=gs, recv_sem=gr.at[z],
+        return pl.ds(pl.multiple_of(128 * o + 64 * lax.rem(t, 2) + 32 * kk, 32), 32)
+
+    def g_copy(p, t, kk):
+        return pltpu.make_async_remote_copy(
+            src_ref=gp.at[p, g_rows(t, kk)], dst_ref=pr.at[p, z], send_sem=gs, recv_sem=gr.at[z],
             device_id=(row_of(xh, 4 * core + t, kk), col), device_id_type=MESH,
         )
 
-    def multiply(o):
-        acc_o = jnp.zeros((128, 512), F32)
-        acc_v = jnp.zeros((128, 512), F32)
+    own = lax.div(z, 4) == core
+    place = lax.rem(z, 4)
+    inner = jnp.logical_or(place == 1, place == 2)
+
+    def nearest(j):
+        t = jnp.where(inner, 1 - j if j < 2 else j, j)
+        return jnp.where(place >= 2, 3 - t, t)
+
+    def multiply(p):
+        acc_o = jnp.zeros((256, 256), F32)
+        acc_v = jnp.zeros((256, 256), F32)
         for b in range(4):
-            acc_o += mdot(rto[o, :, 256 * b : 256 * b + 256], pb[b, :, 0:32, :].reshape(256, 512))
-            acc_v += mdot(rtv[o, :, 128 * b : 128 * b + 128], pb[b, :, 32:48, :].reshape(128, 512))
-        gp[o] = (acc_o * acc_v * SCALE).astype(BF16)
+            left = rto[:, 256 * b : 256 * b + 256]
+            acc_o += mdot(left, pb[p, b, :, 0:32, :].reshape(256, 256))
+            left = rtv[:, 128 * b : 128 * b + 128]
+            acc_v += mdot(left, pb[p, b, :, 32:48, :].reshape(128, 256))
+        gp[p] = (acc_o * acc_v * SCALE).astype(BF16)
+        for j in range(4):
+            t = jnp.where(own, nearest(j), nearest(3 - j))
+            for kk in range(2):
+                mine = row == row_of(xh, 4 * core + t, kk)
+
+                @pl.when(jnp.logical_not(mine))
+                def _():
+                    g_copy(p, t, kk).start()
+
+                @pl.when(mine)
+                def _():
+                    pr[p, z] = gp[p, g_rows(t, kk)]
 
     for dz in NEAR:
-        relay(dz)
+        relay(0, dz)
     for dz in DIST:
         gathered_z(dz)
     for dz in FAR:
-        relay(dz, 0)
+        relay(0, dz)
     for dz in (0, *DIST):
         gathered_x(dz)
+    for dz in (0, *NEAR):
+        forward(0, dz)
+    for dz in NEAR:
+        relay(1, dz)
     for dz in FAR:
-        relay(dz, 1)
-    for dz in (0, *NEAR):
-        forward(dz)
-    for p in range(2):
-        for dz in FAR:
-            forward(dz, p)
+        forward(0, dz)
+    for dz in FAR:
+        relay(1, dz)
     gathered_y(0)
     gathered_y(1)
     pl.semaphore_wait(ready, 16)
-    landed(pb.at[pl.ds(0, 2)], p3r)
+    landed(pb.at[0, pl.ds(0, 2)], p3r.at[0])
     multiply(0)
+    for dz in (0, *DIST):
+        forward(1, dz)
+    landed(pb.at[1, pl.ds(0, 2)], p3r.at[1])
     multiply(1)
-
-    own = lax.div(z, 4) == core
-    place = lax.rem(z, 4)
-    for j in range(4):
-        inner = jnp.logical_or(place == 1, place == 2)
-
-        def nearest(j):
-            t = jnp.where(inner, 1 - j if j < 2 else j, j)
-            return jnp.where(place >= 2, 3 - t, t)
-
-        t = jnp.where(own, nearest(j), nearest(3 - j))
-        for kk in range(2):
-            mine = row == row_of(xh, 4 * core + t, kk)
-
-            @pl.when(jnp.logical_not(mine))
-            def _():
-                g_copy(t, kk).start()
-
-            @pl.when(mine)
-            def _():
-                o = jnp.abs(lax.div(t, 2) - xl)
-                pr[z] = gp[o, pl.ds(pl.multiple_of(64 * lax.rem(t, 2) + 32 * kk, 32), 32)]
 
     slot = 8 * ((1 - xl) * 4 + y)
 
@@ -378,9 +379,9 @@
 
             @pl.when(jnp.logical_or(zs != z, jnp.logical_not(own)))
             def _():
-                landed(pr.at[zs], gr.at[zs])
-
-        part = pr[pl.ds(2 * q, 2)].reshape(64, 512)
+                landed(pr.at[:, zs], gr.at[zs])
+
+        part = jnp.concatenate([pr[p, pl.ds(2 * q, 2)].reshape(64, 256) for p in range(2)], axis=1)
         xs[pl.ds(2 * q, 2)] = mdot(part, mtab[...]).astype(BF16).reshape(2, 32, 1024)
 
         def y_send(j, carry):
@@ -408,11 +409,12 @@
     def _():
         landed(rc.at[0, 0, pl.ds(0, 7)], ras)
 
-    landed(pz.at[pl.ds(0, 7)], p1s)
+    for p in range(2):
+        landed(pz.at[p, pl.ds(0, 7)], p1s)
+        landed(pb.at[p, pl.ds(0, 2)], p2s)
+        landed(pb.at[p, pl.ds(0, 2)], p3s)
     landed(rc.at[0, 0, pl.ds(0, 7)], rbs)
     landed(rc.at[0, 0], rxs)
-    landed(pb.at[pl.ds(0, 2)], p2s)
-    landed(pb.at[pl.ds(0, 2)], p3s)
     landed(rc.at[0, pl.ds(0, 3)], rcs)
     landed(rc.at[1, pl.ds(0, 3)], rcs)
 
@@ -420,7 +422,7 @@
 
     @pl.when(own)
     def _():
-        landed(pr.at[pl.ds(0, 7)], gs)
+        landed(pr.at[:, pl.ds(0, 7)], gs)
 
     @pl.when(jnp.logical_not(own))
     def _():
@@ -469,20 +471,20 @@
             pltpu.VMEM((32, 1024), F32),
             pltpu.VMEM((512, 1024), BF16),
             pltpu.VMEM((256, 256), BF16),
-            pltpu.VMEM((8, 48, 512), BF16),
-            pltpu.VMEM((4, 8, 48, 512), BF16),
+            pltpu.VMEM((2, 8, 48, 256), BF16),
+            pltpu.VMEM((2, 4, 8, 48, 256), BF16),
             pltpu.VMEM((48, 1024), BF16),
             pltpu.VMEM((2, 4, 8, 48, 128), BF16),
-            pltpu.VMEM((2, 128, 1024), BF16),
-            pltpu.VMEM((2, 128, 512), BF16),
-            pltpu.VMEM((2, 128, 512), BF16),
-            pltpu.VMEM((8, 32, 512), BF16),
+            pltpu.VMEM((256, 1024), BF16),
+            pltpu.VMEM((256, 512), BF16),
+            pltpu.VMEM((2, 256, 256), BF16),
+            pltpu.VMEM((2, 8, 32, 256), BF16),
             pltpu.VMEM((8, 32, 1024), BF16),
             pltpu.VMEM((64, 32, 128), BF16),
             dma((6,)),
-            dma, dma((8, 2)),
-            dma, dma((8, 2)),
-            dma, dma,
+            dma, dma((2, 8)),
+            dma, dma((2, 8)),
+            dma, dma((2,)),
             dma, dma,
             dma, dma((8,)),
             dma, dma((8,)),

time: 47.8 us -> 47.1 us (0.985)
  Pallas kernels: 47 us -> 46.4 us
    pallas_call x1, Pallas kernels: 44.9 us -> 44.2 us  [on_device(): pl.pallas_call(kernel, out_shape=pltpu.VMEM((32, 32, 256), F32), in_specs...]
where the time goes in v8:
time: 47.1 us; the launch traced here: 47 us
  Pallas kernels  46.4 us (99%)
  between operations  0.64 us (1%)
    pallas_call x1, Pallas kernels, on_device(): pl.pallas_call(kernel, out_shape=pltpu.VMEM((32, 32, 256), F32), in_specs...  44.2 us
    pallas_call x1, Pallas kernels, on_device(): pl.pallas_call(finish, out_shape=(out, out), in_specs=[vmem], out_specs=(...  2.15 us

profile of v8, /device:TPU:1, one launch (start us, length us, event | category | flops | bytes accessed | tf_op | source)
XLA Modules:
  0.0 47.0 jit_solution(16159548917060314604)
XLA Ops:
  0.6 44.2 %shard_map.77.zb = f32[32,32,256]{2,1,0:T(8,128)S(1)} custom-call(bf16[32,4096]{1,0:T(8,128)(2,1)} %occ.1, bf16[16,4096]{1,0:T(8,128)(2,1)} %vir.1, f32[1,1024]{1,0:T(1,128)} %bitcast.12, f32[1,512]{1,0:T(1,128)} %bitcast.13, f32[32,1024]{1,0:T(8,128)} %constant.4.clone.ctab, bf16[256,256]{1,0:T(8,128)(2,1)} %constant.7.btab), custom_call_target="tpu_custom_call" | custom-call | tf_op jit(solution)/shard_map/pallas_call | solution.py:462
  44.9 2.2 %shard_map.78 = (f32[1024,128]{1,0:T(8,128)}, f32[1024,128]{1,0:T(8,128)}) custom-call(f32[32,32,256]{2,1,0:T(8,128)S(1)} %shard_map.77.zb), custom_call_target="tpu_custom_call" | custom-call | tf_op jit(solution)/shard_map/pallas_call | solution.py:502

commit v9 on v8

--- a/solution.py
+++ b/solution.py
@@ -33,15 +33,15 @@
 
 def b_table():
     cos, sin = angle_table(32)
-    table = np.zeros((2, 2, 16, 4, 2, 4, 32), np.float32)
+    c, s = cos.reshape(2, 2, 8, 32).swapaxes(0, 1), sin.reshape(2, 2, 8, 32).swapaxes(0, 1)
+    table = np.zeros((2, 2, 2, 2, 8, 4, 2, 2, 4, 32), np.float32)
     for kc in range(4):
-        c = cos.reshape(2, 16, 32)
-        s = sin.reshape(2, 16, 32)
-        table[:, 0, :, kc, 0, kc, :] = c
-        table[:, 0, :, kc, 1, kc, :] = -s
-        table[:, 1, :, kc, 0, kc, :] = s
-        table[:, 1, :, kc, 1, kc, :] = c
-    return table.reshape(256, 256)
+        for h in range(2):
+            table[:, :, 0, h, :, kc, h, 0, kc, :] = c
+            table[:, :, 0, h, :, kc, h, 1, kc, :] = -s
+            table[:, :, 1, h, :, kc, h, 0, kc, :] = s
+            table[:, :, 1, h, :, kc, h, 1, kc, :] = c
+    return table.reshape(2, 256, 512)
 
 
 def fft(parts):
@@ -299,7 +299,7 @@
 
     def g_copy(p, t, kk):
         return pltpu.make_async_remote_copy(
-            src_ref=gp.at[p, g_rows(t, kk)], dst_ref=pr.at[p, z], send_sem=gs, recv_sem=gr.at[z],
+            src_ref=gp.at[p, g_rows(t, kk)], dst_ref=pr.at[p, z], send_sem=gs, recv_sem=gr.at[p, z],
             device_id=(row_of(xh, 4 * core + t, kk), col), device_id_type=MESH,
         )
 
@@ -361,45 +361,61 @@
 
     slot = 8 * ((1 - xl) * 4 + y)
 
-    def y_copy(q, c):
+    def y_copy(p, q, c):
         lanes = pl.ds(pl.multiple_of(c * 128, 128), 128)
         return pltpu.make_async_remote_copy(
-            src_ref=xs.at[pl.ds(2 * q, 2), :, lanes], dst_ref=xr.at[pl.ds(slot + 2 * q, 2)],
-            send_sem=ys, recv_sem=yr.at[q], device_id=(row, c), device_id_type=MESH,
+            src_ref=xs.at[p, pl.ds(2 * q, 2), :, lanes], dst_ref=xr.at[p, pl.ds(slot + 2 * q, 2)],
+            send_sem=ys, recv_sem=yr.at[p, q], device_id=(row, c), device_id_type=MESH,
         )
 
     def pair(g):
         near = 3 - 2 * lax.rem(z, 2)
         return lax.rem(lax.div(z, 2) + (0, near, 4 - near, 2)[g], 4)
 
-    for g in range(4):
-        q = pair(g)
-        for t in range(2):
-            zs = 2 * q + t
-
-            @pl.when(jnp.logical_or(zs != z, jnp.logical_not(own)))
-            def _():
-                landed(pr.at[:, zs], gr.at[zs])
-
-        part = jnp.concatenate([pr[p, pl.ds(2 * q, 2)].reshape(64, 256) for p in range(2)], axis=1)
-        xs[pl.ds(2 * q, 2)] = mdot(part, mtab[...]).astype(BF16).reshape(2, 32, 1024)
+    def spread(p, groups):
+        sides = [[], []]
+        for q in groups:
+            for t in range(2):
+                zs = 2 * q + t
+
+                @pl.when(jnp.logical_or(zs != z, jnp.logical_not(own)))
+                def _():
+                    landed(pr.at[p, zs], gr.at[p, zs])
+
+        for q in groups:
+            block = pr[p, pl.ds(2 * q, 2)]
+            for side in range(2):
+                sides[side].append(block[:, 16 * side : 16 * side + 16].reshape(32, 256))
+        both = jnp.concatenate([jnp.concatenate(side, axis=0) for side in sides], axis=1)
+        res = mdot(both, mtab[...]).astype(BF16)
+        for n, q in enumerate(groups):
+            xs[p, pl.ds(2 * q, 2)] = res[32 * n : 32 * n + 32].reshape(2, 16, 1024)
 
         def y_send(j, carry):
-            y_copy(q, lax.rem(col + j, 8)).start()
+            for q in groups:
+                y_copy(p, q, lax.rem(col + j, 8)).start()
             return carry
 
         lax.fori_loop(1, 8, y_send, 0)
         lanes = pl.ds(pl.multiple_of(col * 128, 128), 128)
-        xr[pl.ds(slot + 2 * q, 2)] = xs[pl.ds(2 * q, 2), :, lanes]
-
+        for q in groups:
+            xr[p, pl.ds(slot + 2 * q, 2)] = xs[p, pl.ds(2 * q, 2), :, lanes]
+
+    spread(0, (pair(0), pair(1)))
+    spread(0, (pair(2), pair(3)))
     for g in range(4):
-        q = pair(g)
-        landed(xr.at[pl.ds(0, 14)], yr.at[q])
-        parts = [xr[8 * c + 2 * q + t] for t in range(2) for c in range(8)]
-        both = jnp.concatenate([jnp.concatenate(parts[8 * t : 8 * t + 8], axis=0) for t in range(2)], axis=1)
-        res = mdot(both, ntab[...])
-        for c in range(8):
-            zb[4 * c + q] = res[32 * c : 32 * c + 32]
+        spread(1, (pair(g),))
+
+    for p in range(2):
+        for g in range(4):
+            q = pair(g)
+            landed(xr.at[p, pl.ds(0, 14)], yr.at[p, q])
+            parts = [xr[p, 8 * c + 2 * q + t] for t in range(2) for c in range(8)]
+            both = jnp.concatenate([jnp.concatenate(parts[8 * t : 8 * t + 8], axis=0) for t in range(2)], axis=1)
+            res = mdot(both, ntab[p])
+            for c in range(8):
+                block = res[16 * c : 16 * c + 16]
+                zb[4 * c + q] = block if p == 0 else zb[4 * c + q] + block
 
     @pl.when(jnp.logical_and(col == 0, jnp.logical_not(self_a)))
     def _():
@@ -418,7 +434,8 @@
     landed(rc.at[0, pl.ds(0, 3)], rcs)
     landed(rc.at[1, pl.ds(0, 3)], rcs)
 
-    landed(xr.at[pl.ds(0, 56)], ys)
+    for p in range(2):
+        landed(xr.at[p, pl.ds(0, 56)], ys)
 
     @pl.when(own)
     def _():
@@ -438,8 +455,10 @@
         return pltpu.make_async_copy(res.at[rows], out.at[rows], sem.at[which, i])
 
     def a_step(i, carry):
-        rows = pl.ds(pl.multiple_of(8 * i, 8), 8)
-        res = fft([(zb[a, rows, 0:128], zb[a, rows, 128:256]) for a in range(32)])
+        rows = pl.ds(pl.multiple_of(8 * lax.rem(i, 2), 8), 8)
+        real = pl.ds(pl.multiple_of(256 * lax.div(i, 2), 128), 128)
+        imag = pl.ds(pl.multiple_of(256 * lax.div(i, 2) + 128, 128), 128)
+        res = fft([(zb[a, rows, real], zb[a, rows, imag]) for a in range(32)])
         for j in range(8):
             for part, out in ((0, res_re), (1, res_im)):
                 moved = swap_groups([res[4 * j + t][part] for t in range(4)], lane)
@@ -461,7 +480,7 @@
     dma = pltpu.SemaphoreType.DMA
     zb = pl.pallas_call(
         kernel,
-        out_shape=pltpu.VMEM((32, 32, 256), F32),
+        out_shape=pltpu.VMEM((32, 16, 512), F32),
         in_specs=[anyspace] * 6,
         out_specs=vmem,
         scratch_shapes=[
@@ -470,7 +489,7 @@
             pltpu.VMEM((1, 512), F32),
             pltpu.VMEM((32, 1024), F32),
             pltpu.VMEM((512, 1024), BF16),
-            pltpu.VMEM((256, 256), BF16),
+            pltpu.VMEM((2, 256, 512), BF16),
             pltpu.VMEM((2, 8, 48, 256), BF16),
             pltpu.VMEM((2, 4, 8, 48, 256), BF16),
             pltpu.VMEM((48, 1024), BF16),
@@ -479,8 +498,8 @@
             pltpu.VMEM((256, 512), BF16),
             pltpu.VMEM((2, 256, 256), BF16),
             pltpu.VMEM((2, 8, 32, 256), BF16),
-            pltpu.VMEM((8, 32, 1024), BF16),
-            pltpu.VMEM((64, 32, 128), BF16),
+            pltpu.VMEM((2, 8, 16, 1024), BF16),
+            pltpu.VMEM((2, 64, 16, 128), BF16),
             dma((6,)),
             dma, dma((2, 8)),
             dma, dma((2, 8)),
@@ -489,8 +508,8 @@
             dma, dma((8,)),
             dma, dma((8,)),
             dma, dma((2,)),
-            dma, dma((8,)),
-            dma, dma((4,)),
+            dma, dma((2, 8)),
+            dma, dma((2, 4)),
             pltpu.SemaphoreType.REGULAR,
         ],
         compiler_params=pltpu.CompilerParams(collective_id=0, has_side_effects=True),

time: 47.1 us -> 46.3 us (0.983)
  Pallas kernels: 46.4 us -> 45.6 us
    pallas_call x1, Pallas kernels: 44.2 us -> 43.4 us  [on_device(): pl.pallas_call(kernel, out_shape=pltpu.VMEM((32, 16, 512), F32), in_specs...]
where the time goes in v9:
time: 46.3 us; the launch traced here: 46.2 us
  Pallas kernels  45.6 us (98%)
  between operations  0.64 us (1%)
    pallas_call x1, Pallas kernels, on_device(): pl.pallas_call(kernel, out_shape=pltpu.VMEM((32, 16, 512), F32), in_specs...  43.4 us
    pallas_call x1, Pallas kernels, on_device(): pl.pallas_call(finish, out_shape=(out, out), in_specs=[vmem], out_specs=(...  2.17 us

profile of v9, /device:TPU:1, one launch (start us, length us, event | category | flops | bytes accessed | tf_op | source)
XLA Modules:
  0.0 46.2 jit_solution(14458242740258089749)
XLA Ops:
  0.6 43.4 %shard_map.77.zb = f32[32,16,512]{2,1,0:T(8,128)S(1)} custom-call(bf16[32,4096]{1,0:T(8,128)(2,1)} %occ.1, bf16[16,4096]{1,0:T(8,128)(2,1)} %vir.1, f32[1,1024]{1,0:T(1,128)} %bitcast.12, f32[1,512]{1,0:T(1,128)} %bitcast.13, f32[32,1024]{1,0:T(8,128)} %constant.4.clone.ctab, bf16[2,256,512]{2,1,0:T(8,128)(2,1)} %constant.7.btab), custom_call_target="tpu_custom_call" | custom-call | tf_op jit(solution)/shard_map/pallas_call | solution.py:481
  44.1 2.2 %shard_map.78 = (f32[1024,128]{1,0:T(8,128)}, f32[1024,128]{1,0:T(8,128)}) custom-call(f32[32,16,512]{2,1,0:T(8,128)S(1)} %shard_map.77.zb), custom_call_target="tpu_custom_call" | custom-call | tf_op jit(solution)/shard_map/pallas_call | solution.py:521

commit v10 on v9

--- a/solution.py
+++ b/solution.py
@@ -13,8 +13,7 @@
 F32 = jnp.float32
 BF16 = jnp.bfloat16
 SCALE = -(2.0**-17)
-NEAR, FAR = (1, 7, 2, 6), (3, 5, 4)
-DIST = NEAR + FAR
+DIST = (1, 7, 2, 6, 3, 5, 4)
 
 
 def angle_table(length):
@@ -100,6 +99,17 @@
     def row_of(xh_, z_, k_):
         return (xh_ * 8 + z_) * 2 + k_
 
+    barrier = pltpu.get_barrier_semaphore()
+
+    for i in range(1, 8):
+        pl.semaphore_signal(
+            barrier, inc=1, device_id=(row_of(xh, lax.rem(z + i, 8), core), col), device_id_type=MESH
+        )
+    for i in range(16):
+        pl.semaphore_signal(barrier, inc=1, device_id=(row_of(xh, z, i % 2), i // 2), device_id_type=MESH)
+    for i in range(16):
+        pl.semaphore_signal(barrier, inc=1, device_id=(row_of(1 - xh, z, i % 2), i // 2), device_id_type=MESH)
+
     loads = [
         pltpu.make_async_copy(occ, inb.at[pl.ds(0, 32)], in_sem.at[0]),
         pltpu.make_async_copy(vir, inb.at[pl.ds(32, 16)], in_sem.at[1]),
@@ -111,28 +121,6 @@
     for load in loads:
         load.start()
 
-    barrier = pltpu.get_barrier_semaphore()
-
-    def greet_z(i, c):
-        pl.semaphore_signal(barrier, inc=1, device_id=(row_of(xh, i, core), col), device_id_type=MESH)
-        return c
-
-    def greet_slab(i, c):
-        pl.semaphore_signal(
-            barrier, inc=1, device_id=(row_of(xh, z, lax.rem(i, 2)), lax.div(i, 2)), device_id_type=MESH
-        )
-        return c
-
-    def greet_other(i, c):
-        pl.semaphore_signal(
-            barrier, inc=1, device_id=(row_of(1 - xh, z, lax.rem(i, 2)), lax.div(i, 2)), device_id_type=MESH
-        )
-        return c
-
-    lax.fori_loop(0, 8, greet_z, 0)
-    lax.fori_loop(0, 16, greet_slab, 0)
-    lax.fori_loop(0, 16, greet_other, 0)
-
     for load in loads:
         load.wait()
 
@@ -147,7 +135,7 @@
         dec = jnp.sum(jnp.where(lane == band + 16 * row, dvv[...], 0.0), axis=1, keepdims=True)
         rs[32:48, :] = (inb[32:48, 0:1024].astype(F32) * dec).astype(BF16)
 
-    pl.semaphore_wait(barrier, 40)
+    pl.semaphore_wait(barrier, 39)
 
     def greet_ready(i, c):
         pl.semaphore_signal(
@@ -172,13 +160,13 @@
     def b_copy(dz):
         ref = rc.at[0, y, z]
         return pltpu.make_async_remote_copy(
-            src_ref=ref, dst_ref=ref, send_sem=rbs, recv_sem=rbr.at[z],
+            src_ref=ref, dst_ref=ref, send_sem=rbs, recv_sem=rbr.at[min(dz, 8 - dz) - 1],
             device_id=(row_of(xh, lax.rem(z + dz, 8), core), col), device_id_type=MESH,
         )
 
-    def x_copy(zs):
-        return pltpu.make_async_remote_copy(
-            src_ref=rc.at[0, y, zs], dst_ref=rc.at[1, y, zs], send_sem=rxs, recv_sem=rxr.at[zs],
+    def x_copy(zs, d):
+        return pltpu.make_async_remote_copy(
+            src_ref=rc.at[0, y, zs], dst_ref=rc.at[1, y, zs], send_sem=rxs, recv_sem=rxr.at[d],
             device_id=(row, (1 - xl) * 4 + y), device_id_type=MESH,
         )
 
@@ -196,17 +184,17 @@
     def p1_copy(p, dz):
         zt = lax.rem(z + dz, 8)
         return pltpu.make_async_remote_copy(
-            src_ref=inb.at[:, part_of(zt, p)], dst_ref=pz.at[p, z], send_sem=p1s, recv_sem=p1r.at[p, z],
+            src_ref=inb.at[:, part_of(zt, p)], dst_ref=pz.at[p, z], send_sem=p1s, recv_sem=p1r.at[p, min(dz, 8 - dz) - 1],
             device_id=(row_of(xh, zt, core), col), device_id_type=MESH,
         )
 
     def part_of(zs, p):
         return pl.ds(pl.multiple_of(zs * 512 + p * 256, 256), 256)
 
-    def p2_copy(src, p, zs, side):
+    def p2_copy(src, p, zs, side, d):
         xt = lax.rem(x + 1 + 2 * side, 4)
         return pltpu.make_async_remote_copy(
-            src_ref=src, dst_ref=pb.at[p, 2 * xh + core, zs], send_sem=p2s, recv_sem=p2r.at[p, zs],
+            src_ref=src, dst_ref=pb.at[p, 2 * xh + core, zs], send_sem=p2s, recv_sem=p2r.at[p, d],
             device_id=(row_of(lax.div(xt, 2), z, core), lax.rem(xt, 2) * 4 + y), device_id_type=MESH,
         )
 
@@ -238,7 +226,7 @@
         p1_copy(0, dz).start()
     for p in range(2):
         for side in range(2):
-            p2_copy(inb.at[:, part_of(z, p)], p, z, side).start()
+            p2_copy(inb.at[:, part_of(z, p)], p, z, side, 0).start()
 
     @pl.when(jnp.logical_not(self_a))
     def _():
@@ -247,7 +235,7 @@
     for dz in DIST:
         b_copy(dz).start()
     near_y(0, z)
-    x_copy(z).start()
+    x_copy(z, 0).start()
     for dz in DIST:
         p1_copy(1, dz).start()
 
@@ -264,28 +252,31 @@
     def source(dz):
         return lax.rem(z + 8 - dz, 8)
 
-    def relay(p, dz):
-        zs = source(dz)
-        landed(pz.at[p, zs], p1r.at[p, zs])
-        p2_copy(pz.at[p, zs], p, zs, 0).start()
-        p2_copy(pz.at[p, zs], p, zs, 1).start()
-
-    def forward(p, dz):
-        zs = source(dz)
-        landed(pb.at[p, pl.ds(0, 2), zs], p2r.at[p, zs])
-        p3_copy(p, 0, zs).start()
-        p3_copy(p, 1, zs).start()
-
-    def gathered_z(dz):
-        zs = source(dz)
-        landed(rc.at[0, y, zs], rbr.at[zs])
-        near_y(0, zs)
-        x_copy(zs).start()
-
-    def gathered_x(dz):
-        zs = source(dz)
-        landed(rc.at[1, y, zs], rxr.at[zs])
-        near_y(1, zs)
+    def at(d):
+        return [source(dz) for dz in ((d,) if d in (0, 4) else (d, 8 - d))]
+
+    def relay(p, d):
+        landed(pz.at[p, pl.ds(0, len(at(d)))], p1r.at[p, d - 1])
+        for zs in at(d):
+            for side in range(2):
+                p2_copy(pz.at[p, zs], p, zs, side, d).start()
+
+    def forward(p, d):
+        landed(pb.at[p, 0, pl.ds(0, 2 * len(at(d)))], p2r.at[p, d])
+        for zs in at(d):
+            p3_copy(p, 0, zs).start()
+            p3_copy(p, 1, zs).start()
+
+    def gathered_z(d):
+        landed(rc.at[0, 0, pl.ds(0, len(at(d)))], rbr.at[d - 1])
+        for zs in at(d):
+            x_copy(zs, d).start()
+            near_y(0, zs)
+
+    def gathered_x(d):
+        landed(rc.at[1, 0, pl.ds(0, len(at(d)))], rxr.at[d])
+        for zs in at(d):
+            near_y(1, zs)
 
     def gathered_y(o):
         landed(rc.at[o, pl.ds(0, 3)], rcr.at[o])
@@ -299,7 +290,7 @@
 
     def g_copy(p, t, kk):
         return pltpu.make_async_remote_copy(
-            src_ref=gp.at[p, g_rows(t, kk)], dst_ref=pr.at[p, z], send_sem=gs, recv_sem=gr.at[p, z],
+            src_ref=gp.at[p, g_rows(t, kk)], dst_ref=pr.at[p, z], send_sem=gs, recv_sem=gr.at[p, lax.div(z, 2)],
             device_id=(row_of(xh, 4 * core + t, kk), col), device_id_type=MESH,
         )
 
@@ -333,29 +324,29 @@
                 def _():
                     pr[p, z] = gp[p, g_rows(t, kk)]
 
-    for dz in NEAR:
-        relay(0, dz)
-    for dz in DIST:
-        gathered_z(dz)
-    for dz in FAR:
-        relay(0, dz)
-    for dz in (0, *DIST):
-        gathered_x(dz)
-    for dz in (0, *NEAR):
-        forward(0, dz)
-    for dz in NEAR:
-        relay(1, dz)
-    for dz in FAR:
-        forward(0, dz)
-    for dz in FAR:
-        relay(1, dz)
+    relay(0, 1)
+    relay(0, 2)
+    for d in range(1, 5):
+        gathered_z(d)
+    relay(0, 3)
+    relay(0, 4)
+    for d in range(5):
+        gathered_x(d)
+    for d in range(3):
+        forward(0, d)
+    relay(1, 1)
+    relay(1, 2)
+    forward(0, 3)
+    forward(0, 4)
+    relay(1, 3)
+    relay(1, 4)
     gathered_y(0)
     gathered_y(1)
     pl.semaphore_wait(ready, 16)
     landed(pb.at[0, pl.ds(0, 2)], p3r.at[0])
     multiply(0)
-    for dz in (0, *DIST):
-        forward(1, dz)
+    for d in range(5):
+        forward(1, d)
     landed(pb.at[1, pl.ds(0, 2)], p3r.at[1])
     multiply(1)
 
@@ -375,12 +366,15 @@
     def spread(p, groups):
         sides = [[], []]
         for q in groups:
-            for t in range(2):
-                zs = 2 * q + t
-
-                @pl.when(jnp.logical_or(zs != z, jnp.logical_not(own)))
-                def _():
-                    landed(pr.at[p, zs], gr.at[p, zs])
+            mine = jnp.logical_and(own, q == lax.div(z, 2))
+
+            @pl.when(mine)
+            def _():
+                landed(pr.at[p, 0], gr.at[p, q])
+
+            @pl.when(jnp.logical_not(mine))
+            def _():
+                landed(pr.at[p, pl.ds(0, 2)], gr.at[p, q])
 
         for q in groups:
             block = pr[p, pl.ds(2 * q, 2)]
@@ -446,24 +440,35 @@
         landed(pr, gs)
 
 
-def finish(zb, out_re, out_im, res_re, res_im, sem):
+def finish(zb, out_re, out_im, res_re, res_im, first, second, sem):
     lane = lax.broadcasted_iota(jnp.int32, (8, 128), 1)
 
     def put(i, which):
         res, out = ((res_re, out_re), (res_im, out_im))[which]
-        rows = pl.ds(pl.multiple_of(256 * i, 256), 256)
+        rows = pl.ds(8 * i, 8)
         return pltpu.make_async_copy(res.at[rows], out.at[rows], sem.at[which, i])
 
     def a_step(i, carry):
         rows = pl.ds(pl.multiple_of(8 * lax.rem(i, 2), 8), 8)
         real = pl.ds(pl.multiple_of(256 * lax.div(i, 2), 128), 128)
         imag = pl.ds(pl.multiple_of(256 * lax.div(i, 2) + 128, 128), 128)
-        res = fft([(zb[a, rows, real], zb[a, rows, imag]) for a in range(32)])
-        for j in range(8):
+        for q in range(8):
+            quarter = fft([(zb[8 * n + q, rows, real], zb[8 * n + q, rows, imag]) for n in range(4)])
+            for k in range(4):
+                c, s = math.cos(2 * math.pi * q * k / 32), math.sin(2 * math.pi * q * k / 32)
+                (re, im) = quarter[k]
+                first[k, q, 0] = c * re + s * im if q * k else re
+                first[k, q, 1] = c * im - s * re if q * k else im
+        for k in range(4):
+            eighth = fft([(first[k, q, 0], first[k, q, 1]) for q in range(8)])
+            for j in range(8):
+                second[j, k, 0], second[j, k, 1] = eighth[j]
+        for n in range(4):
             for part, out in ((0, res_re), (1, res_im)):
-                moved = swap_groups([res[4 * j + t][part] for t in range(4)], lane)
-                for kc in range(4):
-                    out[pl.ds(i * 256 + j * 4 + kc, 8, stride=32), :] = moved[kc]
+                moved = []
+                for j in (2 * n, 2 * n + 1):
+                    moved += swap_groups([second[j, t, part] for t in range(4)], lane)
+                out[pl.ds(8 * i, 8), 8 * n : 8 * n + 8, :] = jnp.swapaxes(jnp.stack(moved), 0, 1)
         put(i, 0).start()
         put(i, 1).start()
         return carry
@@ -501,14 +506,14 @@
             pltpu.VMEM((2, 8, 16, 1024), BF16),
             pltpu.VMEM((2, 64, 16, 128), BF16),
             dma((6,)),
-            dma, dma((2, 8)),
-            dma, dma((2, 8)),
+            dma, dma((2, 4)),
+            dma, dma((2, 5)),
             dma, dma((2,)),
             dma, dma,
-            dma, dma((8,)),
-            dma, dma((8,)),
+            dma, dma((4,)),
+            dma, dma((5,)),
             dma, dma((2,)),
-            dma, dma((2, 8)),
+            dma, dma((2, 4)),
             dma, dma((2, 4)),
             pltpu.SemaphoreType.REGULAR,
         ],
@@ -517,15 +522,17 @@
         occ, vir, docc.reshape(1, 1024), dvir.reshape(1, 512),
         jnp.asarray(c_table()), jnp.asarray(b_table()).astype(BF16),
     )
-    out = jax.ShapeDtypeStruct((1024, 128), F32)
+    out = jax.ShapeDtypeStruct((32, 32, 128), F32)
     res = pl.pallas_call(
         finish,
         out_shape=(out, out),
         in_specs=[vmem],
         out_specs=(anyspace, anyspace),
         scratch_shapes=[
-            pltpu.VMEM((1024, 128), F32),
-            pltpu.VMEM((1024, 128), F32),
+            pltpu.VMEM((32, 32, 128), F32),
+            pltpu.VMEM((32, 32, 128), F32),
+            pltpu.VMEM((4, 8, 2, 8, 128), F32),
+            pltpu.VMEM((8, 4, 2, 8, 128), F32),
             dma((2, 4)),
         ],
     )(pltpu.with_memory_space_constraint(zb, pltpu.VMEM))

time: 46.3 us -> 46.1 us (level)
  Pallas kernels: 45.6 us -> 45.1 us
where the time goes in v10:
time: 46.1 us; the launch traced here: 45.7 us
  Pallas kernels  45.1 us (98%)
  between operations  0.64 us (1%)
    pallas_call x1, Pallas kernels, on_device(): pl.pallas_call(kernel, out_shape=pltpu.VMEM((32, 16, 512), F32), in_specs...  43 us
    pallas_call x1, Pallas kernels, on_device(): pl.pallas_call(finish, out_shape=(out, out), in_specs=[vmem], out_specs=(...  2.05 us

profile of v10, /device:TPU:1, one launch (start us, length us, event | category | flops | bytes accessed | tf_op | source)
XLA Modules:
  0.0 45.7 jit_solution(9187089605468801455)
XLA Ops:
  0.6 43.0 %shard_map.77.zb = f32[32,16,512]{2,1,0:T(8,128)S(1)} custom-call(bf16[32,4096]{1,0:T(8,128)(2,1)} %occ.1, bf16[16,4096]{1,0:T(8,128)(2,1)} %vir.1, f32[1,1024]{1,0:T(1,128)} %bitcast.12, f32[1,512]{1,0:T(1,128)} %bitcast.13, f32[32,1024]{1,0:T(8,128)} %constant.4.clone.ctab, bf16[2,256,512]{2,1,0:T(8,128)(2,1)} %constant.7.btab), custom_call_target="tpu_custom_call" | custom-call | tf_op jit(solution)/shard_map/pallas_call | solution.py:486
  43.6 2.0 %shard_map.78 = (f32[32,32,128]{2,1,0:T(8,128)}, f32[32,32,128]{2,1,0:T(8,128)}) custom-call(f32[32,16,512]{2,1,0:T(8,128)S(1)} %shard_map.77.zb), custom_call_target="tpu_custom_call" | custom-call | tf_op jit(solution)/shard_map/pallas_call | solution.py:526

commit v11 on v10

--- a/solution.py
+++ b/solution.py
@@ -224,9 +224,8 @@
 
     for dz in DIST:
         p1_copy(0, dz).start()
-    for p in range(2):
-        for side in range(2):
-            p2_copy(inb.at[:, part_of(z, p)], p, z, side, 0).start()
+    for side in range(2):
+        p2_copy(inb.at[:, part_of(z, 0)], 0, z, side, 0).start()
 
     @pl.when(jnp.logical_not(self_a))
     def _():
@@ -330,6 +329,8 @@
         gathered_z(d)
     relay(0, 3)
     relay(0, 4)
+    for side in range(2):
+        p2_copy(inb.at[:, part_of(z, 1)], 1, z, side, 0).start()
     for d in range(5):
         gathered_x(d)
     for d in range(3):
@@ -343,12 +344,18 @@
     gathered_y(0)
     gathered_y(1)
     pl.semaphore_wait(ready, 16)
-    landed(pb.at[0, pl.ds(0, 2)], p3r.at[0])
-    multiply(0)
-    for d in range(5):
-        forward(1, d)
-    landed(pb.at[1, pl.ds(0, 2)], p3r.at[1])
-    multiply(1)
+    def compute(p, carry):
+        landed(pb.at[p, pl.ds(0, 2)], p3r.at[p])
+        multiply(p)
+
+        @pl.when(p == 0)
+        def _():
+            for d in range(5):
+                forward(1, d)
+
+        return carry
+
+    lax.fori_loop(0, 2, compute, 0)
 
     slot = 8 * ((1 - xl) * 4 + y)
 
@@ -361,7 +368,8 @@
 
     def pair(g):
         near = 3 - 2 * lax.rem(z, 2)
-        return lax.rem(lax.div(z, 2) + (0, near, 4 - near, 2)[g], 4)
+        step = jnp.where(g == 0, 0, jnp.where(g == 1, near, jnp.where(g == 2, 4 - near, 2)))
+        return lax.rem(lax.div(z, 2) + step, 4)
 
     def spread(p, groups):
         sides = [[], []]
@@ -395,13 +403,14 @@
         for q in groups:
             xr[p, pl.ds(slot + 2 * q, 2)] = xs[p, pl.ds(2 * q, 2), :, lanes]
 
-    spread(0, (pair(0), pair(1)))
-    spread(0, (pair(2), pair(3)))
-    for g in range(4):
-        spread(1, (pair(g),))
+    def spread_next(n, carry):
+        spread(lax.div(n, 4), (pair(lax.rem(n, 4)),))
+        return carry
+
+    lax.fori_loop(0, 8, spread_next, 0)
 
     for p in range(2):
-        for g in range(4):
+        def b_step(g, carry):
             q = pair(g)
             landed(xr.at[p, pl.ds(0, 14)], yr.at[p, q])
             parts = [xr[p, 8 * c + 2 * q + t] for t in range(2) for c in range(8)]
@@ -410,6 +419,9 @@
             for c in range(8):
                 block = res[16 * c : 16 * c + 16]
                 zb[4 * c + q] = block if p == 0 else zb[4 * c + q] + block
+            return carry
+
+        lax.fori_loop(0, 4, b_step, 0)
 
     @pl.when(jnp.logical_and(col == 0, jnp.logical_not(self_a)))
     def _():

time: 46.1 us -> 45.4 us (0.985)
  Pallas kernels: 45.1 us -> 44.6 us
where the time goes in v11:
time: 45.4 us; the launch traced here: 45.3 us
  Pallas kernels  44.6 us (98%)
  between operations  0.64 us (1%)
    pallas_call x1, Pallas kernels, on_device(): pl.pallas_call(kernel, out_shape=pltpu.VMEM((32, 16, 512), F32), in_specs...  42.6 us
    pallas_call x1, Pallas kernels, on_device(): pl.pallas_call(finish, out_shape=(out, out), in_specs=[vmem], out_specs=(...  2.05 us

profile of v11, /device:TPU:1, one launch (start us, length us, event | category | flops | bytes accessed | tf_op | source)
XLA Modules:
  0.0 45.3 jit_solution(379961494167336587)
XLA Ops:
  0.6 42.6 %shard_map.77.zb = f32[32,16,512]{2,1,0:T(8,128)S(1)} custom-call(bf16[32,4096]{1,0:T(8,128)(2,1)} %occ.1, bf16[16,4096]{1,0:T(8,128)(2,1)} %vir.1, f32[1,1024]{1,0:T(1,128)} %bitcast.12, f32[1,512]{1,0:T(1,128)} %bitcast.13, f32[32,1024]{1,0:T(8,128)} %constant.4.clone.ctab, bf16[2,256,512]{2,1,0:T(8,128)(2,1)} %constant.7.btab), custom_call_target="tpu_custom_call" | custom-call | tf_op jit(solution)/shard_map/pallas_call | solution.py:498
  43.2 2.0 %shard_map.78 = (f32[32,32,128]{2,1,0:T(8,128)}, f32[32,32,128]{2,1,0:T(8,128)}) custom-call(f32[32,16,512]{2,1,0:T(8,128)S(1)} %shard_map.77.zb), custom_call_target="tpu_custom_call" | custom-call | tf_op jit(solution)/shard_map/pallas_call | solution.py:538

commit v12 on v11

--- a/solution.py
+++ b/solution.py
@@ -475,14 +475,13 @@
             eighth = fft([(first[k, q, 0], first[k, q, 1]) for q in range(8)])
             for j in range(8):
                 second[j, k, 0], second[j, k, 1] = eighth[j]
-        for n in range(4):
-            for part, out in ((0, res_re), (1, res_im)):
+        for part, out in ((0, res_re), (1, res_im)):
+            for n in range(4):
                 moved = []
                 for j in (2 * n, 2 * n + 1):
                     moved += swap_groups([second[j, t, part] for t in range(4)], lane)
                 out[pl.ds(8 * i, 8), 8 * n : 8 * n + 8, :] = jnp.swapaxes(jnp.stack(moved), 0, 1)
-        put(i, 0).start()
-        put(i, 1).start()
+            put(i, part).start()
         return carry
 
     lax.fori_loop(0, 4, a_step, 0)

time: 45.4 us -> 45.3 us (level)
  no operation moved by 1% of the time
where the time goes in v12:
time: 45.3 us; the launch traced here: 45.2 us
  Pallas kernels  44.6 us (98%)
  between operations  0.64 us (1%)
    pallas_call x1, Pallas kernels, on_device(): pl.pallas_call(kernel, out_shape=pltpu.VMEM((32, 16, 512), F32), in_specs...  42.6 us
    pallas_call x1, Pallas kernels, on_device(): pl.pallas_call(finish, out_shape=(out, out), in_specs=[vmem], out_specs=(...  2 us

profile of v12, /device:TPU:1, one launch (start us, length us, event | category | flops | bytes accessed | tf_op | source)
XLA Modules:
  0.0 45.2 jit_solution(14149855284648862396)
XLA Ops:
  0.6 42.6 %shard_map.77.zb = f32[32,16,512]{2,1,0:T(8,128)S(1)} custom-call(bf16[32,4096]{1,0:T(8,128)(2,1)} %occ.1, bf16[16,4096]{1,0:T(8,128)(2,1)} %vir.1, f32[1,1024]{1,0:T(1,128)} %bitcast.12, f32[1,512]{1,0:T(1,128)} %bitcast.13, f32[32,1024]{1,0:T(8,128)} %constant.4.clone.ctab, bf16[2,256,512]{2,1,0:T(8,128)(2,1)} %constant.7.btab), custom_call_target="tpu_custom_call" | custom-call | tf_op jit(solution)/shard_map/pallas_call | solution.py:497
  43.2 2.0 %shard_map.78 = (f32[32,32,128]{2,1,0:T(8,128)}, f32[32,32,128]{2,1,0:T(8,128)}) custom-call(f32[32,16,512]{2,1,0:T(8,128)S(1)} %shard_map.77.zb), custom_call_target="tpu_custom_call" | custom-call | tf_op jit(solution)/shard_map/pallas_call | solution.py:537
